TPU v7x, 256 devices: a whole 4x4x8 slice. The times are simulated.
256 devices in a mesh: copy: 32 (over y, z_lo, core), tok: 8 (over z_hi, x).
Axes of the slice: x: 4, y: 4, z: 8 (z_hi: 2, z_lo: 4; z = z_hi * 4 + z_lo), core: 2. Of those that a mesh axis runs over, the one named last changes fastest.
Arguments:
- noisy: bfloat16 [32, 1024, 768], P('copy', 'tok'), may hold values from -6 to 6
- single: bfloat16 [1024, 768], P('tok'), may hold values from -6 to 6
- pair: bfloat16 [1024, 1024, 128], P('tok', 'copy'), may hold values from -6 to 6
- restype: int32 [1024], P('tok'), may hold values from 0 to 31
- chain: int32 [1024], replicated, may hold values from 0 to 5, never falling along the last dimension, each value on 1 to 512 neighbouring positions
- keymask: int32 [1024], replicated, may hold values from 0 to 1, as said below
- restype_table: bfloat16 [32, 768], replicated, may hold values from -3 to 3
- norm_gain: float32 [768], replicated, may hold values from 0.25 to 1.75
- pair_gain: float32 [128], replicated, may hold values from 0.25 to 1.75
- trans_gain: float32 [768], replicated, may hold values from 0.25 to 1.75
- w_query: bfloat16 [768, 768], replicated, may hold values from -0.21875 to 0.21875
- w_key: bfloat16 [768, 768], replicated, may hold values from -0.21875 to 0.21875
- w_value: bfloat16 [768, 768], replicated, may hold values from -0.21875 to 0.21875
- w_out: bfloat16 [768, 768], replicated, may hold values from -0.21875 to 0.21875
- w_pair: bfloat16 [128, 8], replicated, may hold values from -0.5 to 0.5
- chain_weight: float32 [6, 8], replicated, may hold values from -80 to 240
- w_hidden_gate: bfloat16 [768, 1536], replicated, may hold values from -0.21875 to 0.21875
- w_hidden_up: bfloat16 [768, 1536], replicated, may hold values from -0.21875 to 0.21875
- w_down: bfloat16 [1536, 768], replicated, may hold values from -0.15625 to 0.15625
- cotangent: bfloat16 [32, 1024, 768], P('copy', 'tok'), may hold values from -6 to 6
Outputs:
- grad_noisy: bfloat16 [32, 1024, 768], P('copy', 'tok')
- grad_single: float32 [1024, 768], P('tok', 'copy')
- grad_pair: bfloat16 [1024, 1024, 128], P('tok', 'copy')
- grad_query: float32 [768, 768], P('tok', 'copy')
- grad_key: float32 [768, 768], P('tok', 'copy')
- grad_value: float32 [768, 768], P('tok', 'copy')
- grad_out: float32 [768, 768], P('tok', 'copy')
- grad_pair_weight: float32 [128, 8], replicated
Inputs may be any that keep to these rules, and one draw needn't show every extreme that they name: `keymask`: 1 on the first positions of the crop and 0 after them, with at least 512 ones. chain numbers never fall along the crop.
All inputs are finite; a program needn't handle non-finite values.
Results may differ from a plain program's by a relative error of at most 0.03.
Values may be sent and summed in bfloat16 or wider, within the bound.
A program may use at most 128 MiB of HBM per device.

v0:
```python
import functools

import jax
import jax.numpy as jnp
from jax import lax
from jax.sharding import Mesh
from jax.sharding import PartitionSpec as P

TOK = ("tok_0", "tok_1")
COPY = ("copy_0", "copy_1", "copy_2")
COPY_TOK = ("copy_0", "copy_1", "copy_2", "tok_0", "tok_1")


epsilon = 1e-05
highest_precision = lax.Precision.HIGHEST


def sent_together(arrays, axis, dim, along):
    both = jnp.concatenate(arrays, axis=along)
    filled, at, done = (lax.all_gather(both, axis, axis=dim, tiled=True), 0, [])
    for a in arrays:
        done.append(lax.slice_in_dim(filled, at, at + a.shape[along], axis=along))
        at += a.shape[along]
    return tuple(done)


def sent_to_all(shard, axis):
    count = lax.axis_size(axis)
    return lax.all_to_all(
        jnp.broadcast_to(shard[None], (count, *shard.shape)), axis, 0, 0, tiled=True
    )


def laid_out(blocks, dim):
    dims = list(blocks.shape[1:])
    dims[dim] *= blocks.shape[0]
    return jnp.moveaxis(blocks, 0, dim).reshape(dims)


def gathered_by_axis(shard, axes, dim):
    far, near = axes
    blocks = sent_to_all(sent_to_all(shard, far), near)
    return laid_out(blocks.swapaxes(0, 1).reshape(-1, *shard.shape), dim)


def cut_along(shard, dim, count):
    before, after = (shard.shape[:dim], shard.shape[dim + 1 :])
    return jnp.moveaxis(shard.reshape(*before, count, -1, *after), dim, 0)


def summed_on_arrival(shard, axis, dim):
    blocks = cut_along(shard, dim, lax.axis_size(axis))
    arrived = lax.all_to_all(blocks, axis, split_axis=0, concat_axis=0, tiled=True)
    return arrived.astype(jnp.float32).sum(axis=0)


def summed_rows(shard, axes, dim):
    far, near = axes
    own = summed_on_arrival(cut_along(shard, dim, lax.axis_size(far)), near, dim + 1)
    return jnp.sum(
        lax.all_to_all(own.astype(jnp.bfloat16), far, 0, 0, tiled=True).astype(jnp.float32), axis=0
    )


def by_axis(shard, axes):
    return functools.reduce(lax.psum, axes, shard)


def layer_forward(values, scales):
    average = jnp.mean(values, axis=-1, keepdims=True)
    centred = values - average
    inverse = lax.rsqrt(jnp.mean(centred * centred, axis=-1, keepdims=True) + epsilon)
    normed = centred * inverse
    return (normed * scales, normed, inverse)


def layer_backward(upstream, scales, normed, inverse):
    scaled = upstream * scales
    first_moment = jnp.mean(scaled, axis=-1, keepdims=True)
    second_moment = jnp.mean(scaled * normed, axis=-1, keepdims=True)
    return inverse * (scaled - first_moment - normed * second_moment)


def matmul(left, right):
    return jnp.dot(left, right, preferred_element_type=jnp.float32)


def per_device(
    noisy,
    single,
    pair,
    restype,
    chain,
    keymask,
    restype_table,
    norm_gain,
    pair_gain,
    trans_gain,
    w_query,
    w_key,
    w_value,
    w_out,
    w_pair,
    chain_weight,
    w_hidden_gate,
    w_hidden_up,
    w_down,
    cotangent,
):
    copy_count, tok_rows, model_width = noisy.shape
    head_count = w_pair.shape[1]
    head_width = model_width // head_count
    key_count = chain.shape[0]
    scale = head_width ** (-0.5)
    first_row = lax.axis_index(TOK) * tok_rows
    flat_count = copy_count * tok_rows
    res_onehot = (
        restype[:, None] == jnp.arange(restype_table.shape[0], dtype=jnp.int32)[None, :]
    ).astype(jnp.bfloat16)
    condition = single.astype(jnp.float32) + matmul(res_onehot, restype_table)
    noisy_f = noisy.astype(jnp.float32)
    normed_scaled, noisy_hat, noisy_inverse = layer_forward(noisy_f, norm_gain)
    inputs_x = (normed_scaled + condition[None]).astype(jnp.bfloat16)
    flat_x = inputs_x.reshape(flat_count, model_width)
    query = matmul(flat_x, w_query).astype(jnp.bfloat16).reshape(copy_count, tok_rows, model_width)
    key_local = (
        matmul(flat_x, w_key).astype(jnp.bfloat16).reshape(copy_count, tok_rows, model_width)
    )
    value_local = (
        matmul(flat_x, w_value).astype(jnp.bfloat16).reshape(copy_count, tok_rows, model_width)
    )
    key_full, value_full = sent_together((key_local, value_local), TOK, 1, 0)
    pair_scaled, pair_hat, pair_inverse = layer_forward(pair.astype(jnp.float32), pair_gain)
    pair_rounded = pair_scaled.astype(jnp.bfloat16)
    bias_local = jnp.einsum(
        "ijc,ch->hij", pair_rounded, w_pair, preferred_element_type=jnp.float32
    ).astype(jnp.bfloat16)
    bias_rows = gathered_by_axis(bias_local, (("copy_0", "copy_1"), "copy_2"), 2)
    chain_rows = lax.dynamic_slice_in_dim(chain, first_row, tok_rows)
    chain_onehot = (
        chain[:, None] == jnp.arange(chain_weight.shape[0], dtype=jnp.int32)[None, :]
    ).astype(jnp.float32)
    key_weight = jnp.dot(chain_onehot, chain_weight, precision=highest_precision)
    same_chain = (chain_rows[:, None] == chain[None, :]).astype(jnp.float32)
    extra = bias_rows.astype(jnp.float32) + same_chain[None, :, :] * key_weight.T[:, None, :]
    valid = (keymask > 0)[None, None, None, :]
    query_heads = query.reshape(copy_count, tok_rows, head_count, head_width)
    key_heads = key_full.reshape(copy_count, key_count, head_count, head_width)
    value_heads = value_full.reshape(copy_count, key_count, head_count, head_width)
    logits = (
        jnp.einsum("cihd,cjhd->chij", query_heads, key_heads, preferred_element_type=jnp.float32)
        * scale
        + extra[None]
    )
    logits = jnp.where(valid, logits, -1e30)
    highest = jnp.max(logits, axis=-1, keepdims=True)
    exponent = jnp.exp(logits - highest)
    total_mass = jnp.sum(exponent, axis=-1, keepdims=True)
    weights = exponent / total_mass
    weights_b = weights.astype(jnp.bfloat16)
    attended = jnp.einsum(
        "chij,cjhd->cihd", weights_b, value_heads, preferred_element_type=jnp.float32
    ).astype(jnp.bfloat16)
    flat_att = attended.reshape(flat_count, model_width)
    residual = noisy_f.reshape(flat_count, model_width) + matmul(flat_att, w_out)
    trans_scaled, trans_hat, trans_inverse = layer_forward(residual, trans_gain)
    trans_in = trans_scaled.astype(jnp.bfloat16)
    gate = matmul(trans_in, w_hidden_gate)
    up_part = matmul(trans_in, w_hidden_up)
    sigmoid_gate = jax.nn.sigmoid(gate)
    upstream = cotangent.reshape(flat_count, model_width)
    d_hidden = matmul(upstream, w_down.T)
    d_gate = (d_hidden * up_part * sigmoid_gate * (1.0 + gate * (1.0 - sigmoid_gate))).astype(
        jnp.bfloat16
    )
    d_up = (d_hidden * gate * sigmoid_gate).astype(jnp.bfloat16)
    d_trans = matmul(d_gate, w_hidden_gate.T) + matmul(d_up, w_hidden_up.T)
    d_res = upstream.astype(jnp.float32) + layer_backward(
        d_trans, trans_gain, trans_hat, trans_inverse
    )
    d_res_b = d_res.astype(jnp.bfloat16)
    out_term = jnp.einsum("rd,re->de", flat_att, d_res_b, preferred_element_type=jnp.float32)
    d_att = matmul(d_res_b, w_out.T).astype(jnp.bfloat16).reshape(copy_count, tok_rows, model_width)
    d_att_heads = d_att.reshape(copy_count, tok_rows, head_count, head_width)
    d_weights = jnp.einsum(
        "cihd,cjhd->chij", d_att_heads, value_heads, preferred_element_type=jnp.float32
    )
    delta = jnp.sum(weights * d_weights, axis=-1, keepdims=True)
    d_logits = weights * (d_weights - delta)
    d_logits_b = d_logits.astype(jnp.bfloat16)
    d_query = (
        (
            jnp.einsum("chij,cjhd->cihd", d_logits_b, key_heads, preferred_element_type=jnp.float32)
            * scale
        )
        .astype(jnp.bfloat16)
        .reshape(flat_count, model_width)
    )
    bias_grad_rows = jnp.sum(d_logits, axis=0)
    count = tok_rows * lax.axis_size(TOK)
    key_part = (
        jnp.einsum("chij,cihd->jchd", d_logits_b, query_heads, preferred_element_type=jnp.float32)
        * scale
    )
    value_part = jnp.einsum(
        "chij,cihd->jchd", weights_b, d_att_heads, preferred_element_type=jnp.float32
    )
    key_sums = lax.psum_scatter(
        jnp.concatenate(
            [
                key_part.reshape(count, copy_count, model_width),
                value_part.reshape(count, copy_count, model_width),
            ],
            axis=2,
        ).astype(jnp.bfloat16),
        TOK,
        scatter_dimension=0,
        tiled=True,
    ).astype(jnp.float32)
    d_key = (
        jnp.transpose(key_sums[:, :, :model_width], (1, 0, 2))
        .astype(jnp.bfloat16)
        .reshape(flat_count, model_width)
    )
    d_value = (
        jnp.transpose(key_sums[:, :, model_width:], (1, 0, 2))
        .astype(jnp.bfloat16)
        .reshape(flat_count, model_width)
    )
    d_inputs = matmul(d_query, w_query.T) + matmul(d_key, w_key.T) + matmul(d_value, w_value.T)
    grad_noisy = (
        (
            d_res
            + layer_backward(
                d_inputs,
                norm_gain,
                noisy_hat.reshape(flat_count, model_width),
                noisy_inverse.reshape(flat_count, 1),
            )
        )
        .astype(jnp.bfloat16)
        .reshape(copy_count, tok_rows, model_width)
    )
    grad_single = summed_on_arrival(
        jnp.sum(d_inputs.reshape(copy_count, tok_rows, model_width), axis=0).astype(jnp.bfloat16),
        COPY,
        1,
    )
    bias_grad = summed_rows(
        bias_grad_rows.astype(jnp.bfloat16), (("copy_0", "copy_1"), "copy_2"), 2
    )
    d_pair_scaled = jnp.einsum(
        "hij,ch->ijc", bias_grad, w_pair.astype(jnp.float32), precision=highest_precision
    )
    grad_pair = layer_backward(d_pair_scaled, pair_gain, pair_hat, pair_inverse).astype(
        jnp.bfloat16
    )
    pair_weight_term = jnp.einsum(
        "ijc,hij->ch", pair_rounded.astype(jnp.float32), bias_grad, precision=highest_precision
    )
    grad_pair_weight = by_axis(pair_weight_term, COPY_TOK)
    stacked = jnp.stack(
        [
            jnp.einsum("rd,re->de", flat_x, d_query, preferred_element_type=jnp.float32),
            jnp.einsum("rd,re->de", flat_x, d_key, preferred_element_type=jnp.float32),
            jnp.einsum("rd,re->de", flat_x, d_value, preferred_element_type=jnp.float32),
            out_term,
        ]
    )
    partial_sum = summed_rows(stacked.astype(jnp.bfloat16), (("copy_0", "copy_1"), "copy_2"), 2)
    reduced = summed_on_arrival(partial_sum.astype(jnp.bfloat16), TOK, 1)
    return (
        grad_noisy,
        grad_single,
        grad_pair,
        reduced[0],
        reduced[1],
        reduced[2],
        reduced[3],
        grad_pair_weight,
    )


def solution(mesh):
    torus = Mesh(
        mesh.devices.reshape(4, 4, 2, 2, 4), ("copy_0", "copy_1", "copy_2", "tok_0", "tok_1")
    )
    return jax.shard_map(
        per_device,
        mesh=torus,
        in_specs=(
            P(COPY, TOK, None),
            P(TOK, None),
            P(TOK, COPY, None),
            P(TOK),
            P(),
            P(),
            P(),
            P(),
            P(),
            P(),
            P(),
            P(),
            P(),
            P(),
            P(),
            P(),
            P(),
            P(),
            P(),
            P(COPY, TOK, None),
        ),
        out_specs=(
            P(COPY, TOK, None),
            P(TOK, COPY),
            P(TOK, COPY, None),
            P(TOK, COPY),
            P(TOK, COPY),
            P(TOK, COPY),
            P(TOK, COPY),
            P(),
        ),
        check_vma=False,
    )
```

profile of v0, /device:TPU:24, one launch (start us, length us, event | category | flops | bytes accessed | tf_op | source)
XLA Modules:
  0.0 456.6 jit_solution(11129494750762843628)
XLA Ops:
  13.8 2.0 copy.106
  18.0 8.9 %all-to-all-start = ((bf16[16,8,128,32]{2,3,1,0:T(8,128)(2,1)}), bf16[16,8,128,32]{2,3,1,0:T(8,128)(2,1)}, u32[]{:S(2)}, u32[]{:S(2)}) async-start(bf16[16,8,128,32]{2,3,1,0:T(8,128)(2,1)} %broadcast_in_dim.16), calls=%async_computation | async-start | bytes 2097152 | tf_op jit(solution)/shard_map/all_to_all | solution.py:29
  27.0 2.4 convolution_convert_fusion.7
  32.6 3.6 fusion.57
  36.1 24.8 %all-to-all-done = bf16[16,8,128,32]{2,3,1,0:T(8,128)(2,1)} async-done(((bf16[16,8,128,32]{2,3,1,0:T(8,128)(2,1)}), bf16[16,8,128,32]{2,3,1,0:T(8,128)(2,1)}, u32[]{:S(2)}, u32[]{:S(2)}) %all-to-all-start) | async-done | bytes 1048608 | tf_op jit(solution)/shard_map/all_to_all | solution.py:29
  62.7 5.4 %all_to_all.40 = bf16[2,16,8,128,32]{3,4,1,2,0:T(8,128)(2,1)S(1)} all-to-all(bf16[2,16,8,128,32]{3,4,1,2,0:T(8,128)(2,1)S(1)} %broadcast_in_dim.17), channel_id=1, replica_groups=mesh['copy_0'=4,'copy_1'=4,'copy_2'=2,'tok_0'=2,'tok_1'=4] {'copy_2'}, dimensions={0} | all-to-all | bytes 4194304 | tf_op jit(solution)/shard_map/all_to_all | solution.py:29
  68.7 2.6 copy.110
  71.3 5.3 %copy.111 = f32[8,128,1024]{2,1,0:T(8,128)} copy(f32[8,128,1024]{1,2,0:T(8,128)} %bitcast.200) | data formatting | bytes 8388608 | tf_op jit(solution)/shard_map/convert_element_type | solution.py:145
  76.6 42.2 %all-gather.2.cloned.1.call-done = bf16[2,1024,768]{2,1,0:T(8,128)(2,1)} async-done(((bf16[2,128,768]{2,1,0:T(8,128)(2,1)}), bf16[2,1024,768]{2,1,0:T(8,128)(2,1)}) %all-gather.2.cloned.1.call-update) | async-done | bytes 3145744 | tf_op jit(solution)/shard_map/all_gather | solution.py:20
  118.8 3.7 fusion.72
  122.6 2.6 copy.105
  125.2 2.6 copy.103
  127.8 4.0 add_select_fusion
  131.8 3.2 fusion.75
  135.0 6.7 %convolution_convert_fusion.5 = bf16[8,96,128]{2,1,0:T(8,128)(2,1)} fusion(bf16[1024,8,96]{0,2,1:T(8,128)(2,1)} %bitcast.211, f32[8,128]{1,0:T(8,128)S(1)} %get-tuple-element.66, f32[8,128,1024]{2,1,0:T(8,128)} %copy-done.3), kind=kOutput, calls=%fused_computation.50 | convolution fusion | flops 204572672 | bytes 5967872 | tf_op jit(solution)/shard_map/chij,cjhd->cihd/dot_general | solution.py:161
  141.7 1.8 fusion.76
  145.6 4.3 fusion.21
  149.9 3.4 fusion.71
  154.9 6.8 %convolution_convert_fusion = bf16[8,96,1024]{2,1,0:T(8,128)(2,1)} fusion(bf16[128,8,96]{0,2,1:T(8,128)(2,1)S(1)} %bitcast.220, f32[8,128]{1,0:T(8,128)S(1)} %get-tuple-element.66, f32[8,128,1024]{2,1,0:T(8,128)} %copy-done.3), kind=kOutput, calls=%fused_computation.30 | convolution fusion | flops 205260800 | bytes 5967872 | tf_op jit(solution)/shard_map/chij,cihd->jchd/dot_general | solution.py:205
  161.8 3.2 multiply_reduce_fusion
  167.6 2.0 maximum_bitcast_fusion
  169.6 4.6 %copy.135 = bf16[1024,1536]{1,0:T(8,128)(2,1)} copy(bf16[1024,1536]{0,1:T(8,128)(2,1)} %maximum_bitcast_fusion) | data formatting | bytes 6291456
  174.3 2.4 copy.114
  177.5 2.2 copy.116
  179.7 6.3 %all_to_all.41 = bf16[2,16,8,128,32]{3,4,2,1,0:T(8,128)(2,1)} all-to-all(bf16[2,16,8,128,32]{3,4,2,1,0:T(8,128)(2,1)S(1)} %copy.116), channel_id=1, replica_groups=mesh['copy_0'=4,'copy_1'=4,'copy_2'=2,'tok_0'=2,'tok_1'=4] {'copy_2'}, dimensions={0} | all-to-all | bytes 4194304 | tf_op jit(solution)/shard_map/all_to_all | solution.py:53
  186.0 3.3 reduce_sum.210
  189.3 2.4 fusion.18
  191.7 2.2 fusion.23
  196.1 80.8 %reduce-scatter.4.cloned.1.call-done = bf16[128,1536]{1,0:T(8,128)(2,1)} async-done(((bf16[1024,1536]{1,0:T(8,128)(2,1)}), bf16[128,1536]{1,0:T(8,128)(2,1)}) %reduce-scatter.4.cloned.1.call-update) | async-done | bytes 393232
  280.9 8.6 %all_to_all.42 = bf16[2,16,4,768,24]{3,4,1,2,0:T(8,128)(2,1)} all-to-all(bf16[2,16,4,768,24]{3,4,1,2,0:T(8,128)(2,1)S(1)} %bitcast.199), channel_id=1, replica_groups=mesh['copy_0'=4,'copy_1'=4,'copy_2'=2,'tok_0'=2,'tok_1'=4] {'copy_2'}, dimensions={0} | all-to-all | bytes 9437184 | tf_op jit(solution)/shard_map/all_to_all | solution.py:53
  289.6 5.3 %all-to-all-start.4 = ((bf16[16,8,128,32]{2,3,1,0:T(8,128)(2,1)}), bf16[16,8,128,32]{2,3,1,0:T(8,128)(2,1)}, u32[]{:S(2)}, u32[]{:S(2)}) async-start(bf16[16,8,128,32]{2,3,1,0:T(8,128)(2,1)} %reduce_sum.210), calls=%async_computation.4 | async-start | bytes 2097152 | tf_op jit(solution)/shard_map/all_to_all | solution.py:61
  294.8 3.5 reduce_sum.214
  300.0 20.7 %all-to-all-done.4 = bf16[16,8,128,32]{2,3,1,0:T(8,128)(2,1)} async-done(((bf16[16,8,128,32]{2,3,1,0:T(8,128)(2,1)}), bf16[16,8,128,32]{2,3,1,0:T(8,128)(2,1)}, u32[]{:S(2)}, u32[]{:S(2)}) %all-to-all-start.4) | async-done | bytes 1048608 | tf_op jit(solution)/shard_map/all_to_all | solution.py:61
  320.7 6.0 %all-to-all-start.6 = ((bf16[16,4,768,24]{2,3,1,0:T(8,128)(2,1)}), bf16[16,4,768,24]{2,3,1,0:T(8,128)(2,1)S(1)}, u32[]{:S(2)}, u32[]{:S(2)}) async-start(bf16[16,4,768,24]{2,3,1,0:T(8,128)(2,1)} %copy.123), calls=%async_computation.6 | async-start | bytes 4718592 | tf_op jit(solution)/shard_map/all_to_all | solution.py:61
  326.7 1.9 fusion.77
  330.2 2.8 multiply_reduce_fusion.1
  336.9 43.7 %all-to-all-done.6 = bf16[16,4,768,24]{2,3,1,0:T(8,128)(2,1)S(1)} async-done(((bf16[16,4,768,24]{2,3,1,0:T(8,128)(2,1)}), bf16[16,4,768,24]{2,3,1,0:T(8,128)(2,1)S(1)}, u32[]{:S(2)}, u32[]{:S(2)}) %all-to-all-start.6) | async-done | bytes 2359328 | tf_op jit(solution)/shard_map/all_to_all | solution.py:61
  380.6 6.4 %all-to-all-start.2 = ((bf16[32,128,24]{1,2,0:T(8,128)(2,1)}), bf16[32,128,24]{1,2,0:T(8,128)(2,1)}, u32[]{:S(2)}, u32[]{:S(2)}) async-start(bf16[32,128,24]{1,2,0:T(8,128)(2,1)} %bitcast.218), calls=%async_computation.2 | async-start | bytes 393216 | tf_op jit(solution)/shard_map/all_to_all | solution.py:53
  387.1 3.3 fusion.13
  390.3 2.6 copy.127
  393.0 2.2 reduce_sum.215
  397.7 5.0 %all-to-all-start.7 = ((bf16[8,4,96,24]{2,3,1,0:T(8,128)(2,1)}), bf16[8,4,96,24]{2,3,1,0:T(8,128)(2,1)}, u32[]{:S(2)}, u32[]{:S(2)}) async-start(bf16[8,4,96,24]{2,3,1,0:T(8,128)(2,1)} %copy.124), calls=%async_computation.7 | async-start | bytes 393216 | tf_op jit(solution)/shard_map/all_to_all | solution.py:53
  402.7 2.0 convolution_bitcast_fusion.1
  404.6 7.5 %psum.35 = f32[128,8]{0,1:T(8,128)S(1)} all-reduce(f32[128,8]{0,1:T(8,128)S(1)} %convolution_bitcast_fusion.1), channel_id=1, replica_groups=mesh['copy_0'=4,'copy_1'=4,'copy_2'=2,'tok_0'=2,'tok_1'=4] {'copy_0'}, use_global_device_ids=true, to_apply=%region_22.23 | all-reduce | flops 1024 | bytes 8192 | tf_op jit(solution)/shard_map/psum | solution.py:66
  412.1 11.6 %psum.36 = f32[128,8]{0,1:T(8,128)S(1)} all-reduce(f32[128,8]{0,1:T(8,128)S(1)} %psum.35), channel_id=1, replica_groups=mesh['copy_0'=4,'copy_1'=4,'copy_2'=2,'tok_0'=2,'tok_1'=4] {'copy_1'}, use_global_device_ids=true, to_apply=%region_23.24 | all-reduce | flops 1024 | bytes 8192 | tf_op jit(solution)/shard_map/psum | solution.py:66
  423.8 2.5 psum.37
  426.2 8.8 %psum.38 = f32[128,8]{0,1:T(8,128)S(1)} all-reduce(f32[128,8]{0,1:T(8,128)S(1)} %psum.37), channel_id=1, replica_groups=mesh['copy_0'=4,'copy_1'=4,'copy_2'=2,'tok_0'=2,'tok_1'=4] {'tok_0'}, use_global_device_ids=true, to_apply=%region_25.26 | all-reduce | flops 1024 | bytes 8192 | tf_op jit(solution)/shard_map/psum | solution.py:66
  435.0 11.5 %psum.39 = f32[128,8]{0,1:T(8,128)} all-reduce(f32[128,8]{0,1:T(8,128)S(1)} %psum.38), channel_id=1, replica_groups=mesh['copy_0'=4,'copy_1'=4,'copy_2'=2,'tok_0'=2,'tok_1'=4] {'tok_1'}, use_global_device_ids=true, to_apply=%region_26.27 | all-reduce | flops 1024 | bytes 8192 | tf_op jit(solution)/shard_map/psum | solution.py:66
  (140 shorter events, 40.3 us)
Async XLA Ops:
  7.2 137.1 %copy-start = (bf16[768,1536]{1,0:T(8,128)(2,1)S(1)}, bf16[768,1536]{1,0:T(8,128)(2,1)}, u32[]{:S(2)}) copy-start(bf16[768,1536]{1,0:T(8,128)(2,1)} %param.36) | copy-start | bytes 7077892
  7.2 111.6 %all-gather.2.cloned.1.call-start = ((), (), s32[]{:S(2)}) async-start(), calls=%async_computation.9 | async-start | bytes 3538944 | tf_op jit(solution)/shard_map/all_gather | solution.py:20
  7.2 5.4 %copy-start.13 = (bf16[768,768]{1,0:T(8,128)(2,1)S(1)}, bf16[768,768]{1,0:T(8,128)(2,1)}, u32[]{:S(2)}) copy-start(bf16[768,768]{1,0:T(8,128)(2,1)} %param.31) | copy-start | bytes 3538948
  10.9 2.9 copy-start.5
  13.8 2.6 copy-start.36
  13.8 2.6 copy-start.38
  16.0 371.0 %copy-start.29 = (f32[128,32]{0,1:T(8,128)}, f32[128,32]{0,1:T(8,128)S(1)}, u32[]{:S(2)}) copy-start(f32[128,32]{0,1:T(8,128)S(1)} %broadcast_multiply_fusion.2) | copy-start | bytes 49156
  16.4 370.7 %copy-start.31 = (f32[128,32]{0,1:T(8,128)}, f32[128,32]{0,1:T(8,128)S(1)}, u32[]{:S(2)}) copy-start(f32[128,32]{0,1:T(8,128)S(1)} %add_rsqrt_fusion) | copy-start | bytes 49156
  18.0 13.1 %copy-start.33 = (s32[1024]{0:T(1024)S(1)}, s32[1024]{0:T(1024)}, u32[]{:S(2)}) copy-start(s32[1024]{0:T(1024)} %param.24) | copy-start | bytes 12292
  18.0 13.2 %copy-start.35 = (s32[1024]{0:T(1024)S(1)}, s32[1024]{0:T(1024)}, u32[]{:S(2)}) copy-start(s32[1024]{0:T(1024)} %param.25) | copy-start | bytes 12292
  18.0 13.2 %copy-start.37 = (f32[6,8]{1,0:T(8,128)S(1)}, f32[6,8]{1,0:T(8,128)}, u32[]{:S(2)}) copy-start(f32[6,8]{1,0:T(8,128)} %param.35) | copy-start | bytes 580
  18.0 42.9 %all-to-all-start = ((bf16[16,8,128,32]{2,3,1,0:T(8,128)(2,1)}), bf16[16,8,128,32]{2,3,1,0:T(8,128)(2,1)}, u32[]{:S(2)}, u32[]{:S(2)}) async-start(bf16[16,8,128,32]{2,3,1,0:T(8,128)(2,1)} %broadcast_in_dim.16), calls=%async_computation | async-start | bytes 2097152 | tf_op jit(solution)/shard_map/all_to_all | solution.py:29
  26.9 250.0 %reduce-scatter.4.cloned.1.call-start = ((), (), s32[]{:S(2)}) async-start(), calls=%async_computation.10 | async-start | bytes 3538944
  131.8 3.2 copy-start.3
  141.7 2.6 copy-start.34
  143.5 0.8 copy-start.7
  149.9 3.4 copy-start.8
  149.9 3.4 copy-start.26
  149.9 4.3 copy-start.12
  154.2 7.6 %copy-start.16 = (f32[128,768]{1,0:T(8,128)}, f32[128,768]{1,0:T(8,128)S(1)}, u32[]{:S(2)}) copy-start(f32[128,768]{1,0:T(8,128)S(1)} %get-tuple-element.55) | copy-start | bytes 1179652
  154.9 6.9 %copy-start.24 = (bf16[1,1024,768]{1,2,0:T(8,128)(2,1)S(1)}, bf16[1,1024,768]{1,2,0:T(8,128)(2,1)}, u32[]{:S(2)}) copy-start(bf16[1,1024,768]{1,2,0:T(8,128)(2,1)} %copy.103) | copy-start | bytes 4718596
  161.8 3.5 copy-start.2
  165.2 0.9 copy-start.23
  166.2 1.4 copy-start.25
  174.2 2.4 copy-start.28
  186.0 3.3 copy-start.27
  191.7 2.9 copy-start.6
  194.0 0.7 copy-start.20
  278.2 1.4 copy-start.10
  278.2 1.8 copy-start.11
  278.2 2.3 copy-start.18
  278.2 2.3 copy-start.21
  289.6 31.2 %all-to-all-start.4 = ((bf16[16,8,128,32]{2,3,1,0:T(8,128)(2,1)}), bf16[16,8,128,32]{2,3,1,0:T(8,128)(2,1)}, u32[]{:S(2)}, u32[]{:S(2)}) async-start(bf16[16,8,128,32]{2,3,1,0:T(8,128)(2,1)} %reduce_sum.210), calls=%async_computation.4 | async-start | bytes 2097152 | tf_op jit(solution)/shard_map/all_to_all | solution.py:61
  320.7 59.9 %all-to-all-start.6 = ((bf16[16,4,768,24]{2,3,1,0:T(8,128)(2,1)}), bf16[16,4,768,24]{2,3,1,0:T(8,128)(2,1)S(1)}, u32[]{:S(2)}, u32[]{:S(2)}) async-start(bf16[16,4,768,24]{2,3,1,0:T(8,128)(2,1)} %copy.123), calls=%async_computation.6 | async-start | bytes 4718592 | tf_op jit(solution)/shard_map/all_to_all | solution.py:61
  328.6 4.3 copy-start.14
  328.6 4.3 copy-start.19
  330.1 2.8 copy-start.30
  330.1 3.4 copy-start.9
  330.1 3.4 copy-start.15
  330.2 3.4 copy-start.22
  330.2 3.4 copy-start.32
  333.0 1.3 copy-start.17
  380.6 9.7 %copy-start.4 = (bf16[16,4,768,24]{2,3,1,0:T(8,128)(2,1)}, bf16[16,4,768,24]{2,3,1,0:T(8,128)(2,1)S(1)}, u32[]{:S(2)}) copy-start(bf16[16,4,768,24]{2,3,1,0:T(8,128)(2,1)S(1)} %all-to-all-done.6) | copy-start | bytes 7077892
  380.6 17.1 %all-to-all-start.2 = ((bf16[32,128,24]{1,2,0:T(8,128)(2,1)}), bf16[32,128,24]{1,2,0:T(8,128)(2,1)}, u32[]{:S(2)}, u32[]{:S(2)}) async-start(bf16[32,128,24]{1,2,0:T(8,128)(2,1)} %bitcast.218), calls=%async_computation.2 | async-start | bytes 393216 | tf_op jit(solution)/shard_map/all_to_all | solution.py:53
  393.0 56.7 %copy-start.1 = (bf16[768,1536]{1,0:T(8,128)(2,1)S(1)}, bf16[768,1536]{1,0:T(8,128)(2,1)}, u32[]{:S(2)}) copy-start(bf16[768,1536]{1,0:T(8,128)(2,1)} %param.36) | copy-start | bytes 7077892
  397.7 50.4 %all-to-all-start.7 = ((bf16[8,4,96,24]{2,3,1,0:T(8,128)(2,1)}), bf16[8,4,96,24]{2,3,1,0:T(8,128)(2,1)}, u32[]{:S(2)}, u32[]{:S(2)}) async-start(bf16[8,4,96,24]{2,3,1,0:T(8,128)(2,1)} %copy.124), calls=%async_computation.7 | async-start | bytes 393216 | tf_op jit(solution)/shard_map/all_to_all | solution.py:53
Sparse Core Ops, SparseCore 0:
  13.9 104.8 all-gather.1
  174.4 102.5 reduce-scatter.3
where the time goes:
time: 460 us; the launch traced here: 457 us
  waiting for transfers between devices  212 us (46%)
  blocking collectives  62.2 us (14%)
  matrix products  57.8 us (13%)
  local copies, waits for them, and re-layouts  48.1 us (10%)
  starting transfers between devices  31.6 us (7%)
  other arithmetic  29.9 us (6%)
  between operations  14.7 us (3%)
    unnamed x3, waiting for transfers between devices  80.9 us
    all_to_all x2, waiting for transfers between devices, summed_rows(): lax.all_to_all(own.astype(jnp.bfloat16), far, 0, 0, tiled=True)  64.5 us
    all_gather x1, waiting for transfers between devices, sent_together(): filled, at, done = (lax.all_gather(both, axis, axis=dim, tiled=True), 0, [])  42.2 us
    psum x5, blocking collectives, by_axis(): return functools.reduce(lax.psum, axes, shard)  41.9 us
    all_to_all x1, waiting for transfers between devices, sent_to_all(): lax.all_to_all(jnp.broadcast_to(shard[None], (count, *shard.shape)), axis...  24.8 us
    dot_general x13, matrix products, matmul(): return jnp.dot(left, right, preferred_element_type=jnp.float32)  23.8 us
    all_to_all x2, blocking collectives, summed_on_arrival(): lax.all_to_all(blocks, axis, split_axis=0, concat_axis=0, tiled=True)  14.9 us
    unnamed x82, local copies, waits for them, and re-layouts  13.9 us
  transfers between devices with their start and end apart: 7, of which 5 were waited for; matrix products, arithmetic and copies ran while one was open for 15% of the time, Pallas kernels for 0%

commit v1 on v0

v1 whole, which is shorter than its diff:
```python
import jax
import jax.numpy as jnp
from jax import lax
from jax.experimental import pallas as pl
from jax.experimental.pallas import tpu as pltpu
from jax.sharding import Mesh
from jax.sharding import PartitionSpec as P

TOK = ("tok_0", "tok_1")
COPY = ("copy_0", "copy_1", "copy_2")
MESH = pl.DeviceIdType.MESH
VM = pl.BlockSpec(memory_space=pltpu.VMEM)
BF = jnp.bfloat16
F32 = jnp.float32
epsilon = 1e-05


def dot(a, b, ca=1, cb=0):
    return lax.dot_general(a, b, (((ca,), (cb,)), ((), ())), preferred_element_type=F32)


class Place:
    def __init__(self):
        self.y = lax.axis_index("copy_0")
        self.z = lax.axis_index("copy_1")
        self.core = lax.axis_index("copy_2")
        self.zh = lax.axis_index("tok_0")
        self.x = lax.axis_index("tok_1")
        self.tok = self.zh * 4 + self.x
        self.chip = self.y * 4 + self.z
        self.copy = self.chip * 2 + self.core

    def around_y(self, d):
        return {"copy_0": lax.rem(self.y + d, 4)}

    def around_z(self, d):
        return {"copy_1": lax.rem(self.z + d, 4)}

    def around_x(self, d):
        return {"tok_1": lax.rem(self.x + d, 4)}

    def other_core(self):
        return {"copy_2": 1 - self.core}

    def other_half(self):
        return {"tok_0": 1 - self.zh}

    def tok_at(self, d):
        t = lax.rem(self.tok + d, 8)
        return t, {"tok_0": t // 4, "tok_1": lax.rem(t, 4)}


class Wire:
    def __init__(self, send, recv):
        self.send, self.recv, self.at, self.open = send, recv, 0, []

    def go(self, src, dst, device):
        c = pltpu.make_async_remote_copy(
            src_ref=src,
            dst_ref=dst,
            send_sem=self.send.at[self.at],
            recv_sem=self.recv.at[self.at],
            device_id=device,
            device_id_type=MESH,
        )
        self.at += 1
        c.start()
        self.open.append(c)
        return c

    def close(self):
        for c in self.open:
            c.wait_send()


def greet(devices, more=0):
    barrier = pltpu.get_barrier_semaphore()
    for d in devices:
        pl.semaphore_signal(barrier, inc=1, device_id=d, device_id_type=MESH)
    pl.semaphore_wait(barrier, len(devices) + more)


def gather_tok(w, me, src, out, rows):
    half = rows // 2
    zc = w.go(src, out.at[me.tok], me.other_half())

    def ring_start(unit_src, slot):
        left = w.go(unit_src, out.at[slot], me.around_x(3))
        right = w.go(unit_src, out.at[slot], me.around_x(1))
        return left, right

    def ring_pass(pair, zh):
        left, right = pair
        from_left = zh * 4 + lax.rem(me.x + 3, 4)
        from_right = zh * 4 + lax.rem(me.x + 1, 4)
        right.wait_recv()
        a = w.go(
            out.at[from_left, pl.ds(0, half)], out.at[from_left, pl.ds(0, half)], me.around_x(1)
        )
        left.wait_recv()
        b = w.go(
            out.at[from_right, pl.ds(half, half)],
            out.at[from_right, pl.ds(half, half)],
            me.around_x(3),
        )
        return a, b

    own = ring_start(src, me.tok)
    own_far = ring_pass(own, me.zh)
    zc.wait_recv()
    oz = 1 - me.zh
    far_slot = oz * 4 + me.x
    far = ring_start(out.at[far_slot], far_slot)
    far_far = ring_pass(far, oz)
    return own_far + far_far


def add_into(dst, a, b):
    dst[...] = (a[...].astype(F32) + b[...].astype(F32)).astype(dst.dtype)


def scatter_sum(w, me, s, near_a, near_b, from_l, from_r, from_z):
    opp = lax.rem(me.y + 2, 4) * 4
    lo = lax.rem(me.y + 3, 4) * 4
    hi = lax.rem(me.y + 1, 4) * 4
    a = w.go(s.at[pl.ds(opp, 2)], near_a, me.around_y(3))
    b = w.go(s.at[pl.ds(opp + 2, 2)], near_b, me.around_y(1))
    a.wait_recv()
    add_into(s.at[pl.ds(lo, 2)], s.at[pl.ds(lo, 2)], near_a)
    c = w.go(s.at[pl.ds(lo, 4)], from_r, me.around_y(3))
    b.wait_recv()
    add_into(s.at[pl.ds(hi + 2, 2)], s.at[pl.ds(hi + 2, 2)], near_b)
    d = w.go(s.at[pl.ds(hi, 4)], from_l, me.around_y(1))
    c.wait_recv()
    d.wait_recv()
    own = s.at[pl.ds(me.y * 4, 4)]
    own[...] = (
        own[...].astype(F32) + from_l[...].astype(F32) + from_r[...].astype(F32)
    ).astype(own.dtype)
    zs = []
    for k in (1, 2, 3):
        zt = lax.rem(me.z + k, 4)
        zs.append(w.go(s.at[me.y * 4 + zt], from_z.at[k - 1], me.around_z(k)))
    for k in zs:
        k.wait_recv()
    total = s[me.chip].astype(F32)
    for k in range(3):
        total = total + from_z[k].astype(F32)
    return total


def scatter_scratch(rest):
    return [
        pltpu.VMEM((2, *rest), BF),
        pltpu.VMEM((2, *rest), BF),
        pltpu.VMEM((4, *rest), BF),
        pltpu.VMEM((4, *rest), BF),
        pltpu.VMEM((3, *rest), BF),
    ]


def sems(n):
    return [pltpu.SemaphoreType.DMA((n,)), pltpu.SemaphoreType.DMA((n,))]


def comm_call(kernel, outs, scratch, cid, args):
    return pl.pallas_call(
        kernel,
        out_shape=outs,
        in_specs=[VM] * len(args),
        out_specs=[VM] * len(outs),
        scratch_shapes=scratch,
        compiler_params=pltpu.CompilerParams(
            collective_id=cid, has_side_effects=True, vmem_limit_bytes=48 << 20
        ),
    )(*args)


def spread_kernel(x, bt, xf, f, send, recv):
    me = Place()
    w = Wire(send, recv)
    toks = [me.tok_at(d) for d in range(1, 8)]
    greet(
        [d for _, d in toks]
        + [me.other_core()]
        + [me.around_z(k) for k in (1, 2, 3)]
        + [me.around_y(k) for k in (1, 3)]
    )
    heads = [w.go(bt.at[t], f.at[me.copy, me.tok], d) for t, d in toks]
    xf[me.tok] = x[...]
    f[me.copy, me.tok] = bt[me.tok]
    for h in heads:
        h.wait_recv()
    mine = pl.ds(4 * me.core, 4)
    theirs = pl.ds(4 * (1 - me.core), 4)
    first = w.go(f.at[me.copy, theirs], f.at[me.copy, theirs], me.other_core())
    first.wait_recv()
    last = [w.go(f.at[me.copy, mine], f.at[me.copy, mine], me.other_core())]
    chip = f.at[pl.ds(me.chip * 2, 2), mine]
    zs = [w.go(chip, chip, me.around_z(k)) for k in (1, 2, 3)]
    tail = gather_tok(w, me, x, xf, 128)
    for k, c in zip((1, 2, 3), zs):
        c.wait_recv()
        src = f.at[pl.ds((me.y * 4 + lax.rem(me.z + 4 - k, 4)) * 2, 2), mine]
        last.append(w.go(src, src, me.other_core()))
    row = f.at[pl.ds(me.y * 8, 8), mine]
    left = w.go(row, row, me.around_y(3))
    right = w.go(row, row, me.around_y(1))
    lo = lax.rem(me.y + 3, 4) * 8
    hi = lax.rem(me.y + 1, 4) * 8
    op = lax.rem(me.y + 2, 4) * 8
    right.wait_recv()
    src = f.at[pl.ds(lo, 4), mine]
    a = w.go(src, src, me.around_y(1))
    src = f.at[pl.ds(lo, 8), mine]
    last.append(w.go(src, src, me.other_core()))
    left.wait_recv()
    src = f.at[pl.ds(hi + 4, 4), mine]
    b = w.go(src, src, me.around_y(3))
    src = f.at[pl.ds(hi, 8), mine]
    last.append(w.go(src, src, me.other_core()))
    a.wait_recv()
    src = f.at[pl.ds(op, 4), mine]
    last.append(w.go(src, src, me.other_core()))
    b.wait_recv()
    src = f.at[pl.ds(op + 4, 4), mine]
    last.append(w.go(src, src, me.other_core()))
    for c in last:
        c.wait_recv()
    for c in tail:
        c.wait_recv()
    w.close()


def spread(x, bt):
    return comm_call(
        spread_kernel,
        [
            jax.ShapeDtypeStruct((8, 128, 768), BF),
            jax.ShapeDtypeStruct((32, 8, 32, 128), BF),
        ],
        sems(40),
        0,
        (x, bt),
    )


def exchange_kernel(a, o, send, recv):
    me = Place()
    w = Wire(send, recv)
    toks = [me.tok_at(d) for d in range(1, 8)]
    greet([d for _, d in toks])
    moves = [w.go(a.at[t], o.at[me.tok], d) for t, d in toks]
    o[me.tok] = a[me.tok]
    for c in moves:
        c.wait_recv()
    w.close()


def exchange(a):
    return comm_call(exchange_kernel, [jax.ShapeDtypeStruct(a.shape, BF)], sems(8), 1, (a,))[0]


def gather_kernel(a, o, send, recv):
    me = Place()
    w = Wire(send, recv)
    greet([me.other_half(), me.around_x(1), me.around_x(3)])
    o[me.tok] = a[...]
    for c in gather_tok(w, me, a, o, 768):
        c.wait_recv()
    w.close()


def gather(a):
    return comm_call(
        gather_kernel, [jax.ShapeDtypeStruct((8, *a.shape), BF)], sems(12), 2, (a,)
    )[0]


def home_kernel(
    dq, db, wg, odq, odb, owg, send, recv, db1, s1, wg1, ws, bl, bu, gt, *bufs
):
    me = Place()
    w = Wire(send, recv)
    bufs_w, bufs_d = bufs[:5], bufs[5:]
    toks = [me.tok_at(d) for d in range(1, 8)]
    turn = me.tok * 4 + lax.rem(me.copy, 4)
    turn_tok = me.copy // 4
    other = turn_tok != me.tok
    partner = {
        "copy_0": turn // 8,
        "copy_1": lax.rem(turn // 2, 4),
        "copy_2": lax.rem(turn, 2),
        "tok_0": turn_tok // 4,
        "tok_1": lax.rem(turn_tok, 4),
    }
    barrier = pltpu.get_barrier_semaphore()

    @pl.when(other)
    def _():
        pl.semaphore_signal(barrier, inc=1, device_id=partner, device_id_type=MESH)

    greet(
        [d for _, d in toks]
        + [me.other_core()]
        + [me.around_z(k) for k in (1, 2, 3)]
        + [me.around_y(k) for k in (1, 3)],
        jnp.where(other, 1, 0),
    )
    mine = pl.ds(4 * me.core, 4)
    theirs = pl.ds(4 * (1 - me.core), 4)
    cw = w.go(wg.at[1 - me.core], wg1, me.other_core())
    cb = w.go(db.at[:, :, theirs], db1, me.other_core())
    moves = [w.go(dq.at[t], odq.at[:, me.tok], d) for t, d in toks]
    odq[:, me.tok] = dq[me.tok]
    cw.wait_recv()
    ws[...] = (wg[me.core].astype(F32) + wg1[...].astype(F32)).astype(BF)
    cb.wait_recv()

    @pl.loop(0, 16)
    def _(c):
        s1[c] = (db[c, :, mine].astype(F32) + db1[c].astype(F32)).astype(BF)

    total = scatter_sum(w, me, ws, *bufs_w)
    gt[...] = total.astype(BF)
    owg[3] = gt[3]
    k = w.at
    w.at += 1

    def turned():
        return pltpu.make_async_remote_copy(
            src_ref=gt.at[pl.ds(0, 3)],
            dst_ref=owg.at[pl.ds(0, 3)],
            send_sem=send.at[k],
            recv_sem=recv.at[k],
            device_id=partner,
            device_id_type=MESH,
        )

    @pl.when(other)
    def _():
        turned().start()

    @pl.when(jnp.logical_not(other))
    def _():
        owg[pl.ds(0, 3)] = gt[pl.ds(0, 3)]

    total = scatter_sum(w, me, s1, *bufs_d)
    bu[...] = total.astype(BF)
    back = w.go(bu.at[1 - me.core], bl.at[mine], me.other_core())
    bl[mine] = bu[me.core]
    back.wait_recv()
    fan = [w.go(bl.at[t], odb.at[me.tok], d) for t, d in toks]
    odb[me.tok] = bl[me.tok]
    for c in moves + fan:
        c.wait_recv()

    @pl.when(other)
    def _():
        turned().wait()

    w.close()


def home(dq, db, wg):
    return comm_call(
        home_kernel,
        [
            jax.ShapeDtypeStruct((3, 8, 96, 128), BF),
            jax.ShapeDtypeStruct((8, 32, 128), BF),
            jax.ShapeDtypeStruct((4, 24, 128), BF),
        ],
        sems(40)
        + [
            pltpu.VMEM((16, 2, 4, 32, 128), BF),
            pltpu.VMEM((16, 2, 4, 32, 128), BF),
            pltpu.VMEM((16, 4, 24, 128), BF),
            pltpu.VMEM((16, 4, 24, 128), BF),
            pltpu.VMEM((8, 32, 128), BF),
            pltpu.VMEM((2, 4, 32, 128), BF),
            pltpu.VMEM((4, 24, 128), BF),
        ]
        + scatter_scratch((4, 24, 128))
        + scatter_scratch((2, 4, 32, 128)),
        3,
        (dq, db, wg),
    )


def finish_kernel(gs, pw, ogs, opw, send, recv, gs1, ss, p0, p1, p2, p3, r0, r1, r2, r3, *bufs):
    me = Place()
    w = Wire(send, recv)
    toks = [me.tok_at(d) for d in range(1, 8)]
    greet(
        [d for _, d in toks]
        + [me.other_core()]
        + [me.around_z(k) for k in (1, 2, 3)]
        + [me.around_y(k) for k in (1, 2, 3)]
    )
    cg = w.go(gs.at[1 - me.core], gs1, me.other_core())
    c0 = w.go(pw, r0, me.other_core())
    c0.wait_recv()
    p0[...] = pw[...] + r0[...]
    zs = [w.go(p0, r1.at[k - 1], me.around_z(k)) for k in (1, 2, 3)]
    cg.wait_recv()
    ss[...] = (gs[me.core].astype(F32) + gs1[...].astype(F32)).astype(BF)
    for c in zs:
        c.wait_recv()
    z = me.z

    def in_order(own, got, at):
        terms = []
        for k in range(4):
            d = lax.rem(at + 4 - k, 4)
            term = jnp.where(d == 0, own[...], jnp.zeros_like(own[...]))
            for j in (1, 2, 3):
                term = jnp.where(d == j, got[j - 1], term)
            terms.append(term)
        return (terms[0] + terms[1]) + (terms[2] + terms[3])

    p1[...] = in_order(p0, r1, z)
    ys = [w.go(p1, r2.at[k - 1], me.around_y(k)) for k in (1, 2, 3)]
    for c in ys:
        c.wait_recv()
    p2[...] = in_order(p1, r2, me.y)
    ts = [w.go(p2, r3.at[me.tok], d) for _, d in toks]
    r3[me.tok] = p2[...]
    ogs[...] = scatter_sum(w, me, ss, *bufs)
    for c in ts:
        c.wait_recv()
    total = r3[0]
    for k in range(1, 8):
        total = total + r3[k]
    opw[...] = total
    w.close()


def finish(gs, pw):
    return comm_call(
        finish_kernel,
        [jax.ShapeDtypeStruct((24, 128), F32), jax.ShapeDtypeStruct((8, 128), F32)],
        sems(32)
        + [
            pltpu.VMEM((16, 24, 128), BF),
            pltpu.VMEM((16, 24, 128), BF),
            pltpu.VMEM((8, 128), F32),
            pltpu.VMEM((8, 128), F32),
            pltpu.VMEM((8, 128), F32),
            pltpu.VMEM((8, 128), F32),
            pltpu.VMEM((8, 128), F32),
            pltpu.VMEM((3, 8, 128), F32),
            pltpu.VMEM((3, 8, 128), F32),
            pltpu.VMEM((8, 8, 128), F32),
        ]
        + scatter_scratch((24, 128)),
        4,
        (gs, pw),
    )


def forward_kernel(
    xf, wq, wk, wv, f, same, diff, chj, chi, att, pt, q, k, v, ab, bb, cb, vt
):
    h = lax.axis_index("tok_0") * 4 + lax.axis_index("tok_1")
    row = lax.broadcasted_iota(jnp.int32, (768, 128), 0)
    col = lax.broadcasted_iota(jnp.int32, (768, 128), 1)
    pick = jnp.where((row == col + h * 96) & (col < 96), 1.0, 0.0).astype(BF)
    ws = [dot(m[...], pick).astype(BF) for m in (wq, wk, wv)]
    for t in range(8):
        xt = xf[t]
        for m, o in zip(ws, (q, k, v)):
            o[t * 128 : (t + 1) * 128] = dot(xt, m).astype(BF)
    vt[...] = v[...].T
    ab[...] = jnp.broadcast_to(same[...], (1024, 128))
    bb[...] = jnp.broadcast_to(diff[...], (1024, 128))
    cb[...] = jnp.broadcast_to(chj[...], (1024, 128))
    scale = 96**-0.5

    @pl.loop(0, 8)
    def _(t):
        rows = pl.ds(pl.multiple_of(t * 128, 128), 128)
        s = dot(k[...], q[rows], 1, 1)
        bias = f[:, t].reshape(1024, 128).astype(F32)
        s = s * scale + (bias + jnp.where(cb[...] == chi[t], ab[...], bb[...]))
        e = jnp.exp(s - jnp.max(s, axis=0, keepdims=True))
        p = (e * (1.0 / jnp.sum(e, axis=0, keepdims=True))).astype(BF)
        pt[t] = p
        att[t] = dot(vt[...], p)[:96].astype(BF)


def forward(xf, wq, wk, wv, f, same, diff, chj, chi):
    args = (xf, wq, wk, wv, f, same, diff, chj, chi)
    return pl.pallas_call(
        forward_kernel,
        out_shape=[
            jax.ShapeDtypeStruct((8, 96, 128), BF),
            jax.ShapeDtypeStruct((8, 1024, 128), BF),
            jax.ShapeDtypeStruct((1024, 128), BF),
            jax.ShapeDtypeStruct((1024, 128), BF),
            jax.ShapeDtypeStruct((1024, 128), BF),
        ],
        in_specs=[VM] * len(args),
        out_specs=[VM] * 5,
        scratch_shapes=[
            pltpu.VMEM((1024, 128), F32),
            pltpu.VMEM((1024, 128), F32),
            pltpu.VMEM((1024, 128), jnp.int32),
            pltpu.VMEM((128, 1024), BF),
        ],
        compiler_params=pltpu.CompilerParams(vmem_limit_bytes=48 << 20),
    )(*args)


def backward_kernel(
    xf, q, k, v, pt, dr, att, wo, dq, db, wg, kt, dk, dv, go, z
):
    kt[...] = k[...].T
    dk[...] = jnp.zeros_like(dk)
    dv[...] = jnp.zeros_like(dv)
    go[...] = jnp.zeros_like(go)
    scale = 96**-0.5

    @pl.loop(0, 8)
    def _(t):
        rows = pl.ds(pl.multiple_of(t * 128, 128), 128)
        d_att = dot(wo[...], dr[t])
        d_att_b = d_att.astype(BF)
        p = pt[t]
        dp = dot(v[...], d_att_b)
        pf = p.astype(F32)
        ds = pf * (dp - jnp.sum(pf * dp, axis=0, keepdims=True))
        dsb = ds.astype(BF)
        db[:, :, t] = dsb.reshape(16, 2, 32, 128)
        dqt = (dot(kt[...], dsb)[:96] * scale).astype(BF)
        dq[t, 0] = dqt
        z[0:96, rows] = dqt
        dv[...] += dot(p, d_att.T.astype(BF))
        dk[...] += dot(dsb, q[rows])
        a = att[t].astype(F32).T.astype(BF)
        go[...] += dot(dr[t], a)

    dkt = (dk[...] * scale).T[:96].astype(BF)
    dvt = dv[...].T[:96].astype(BF)
    z[96:192] = dkt
    z[192:288] = dvt
    for t in range(8):
        dq[t, 1] = dkt[:, t * 128 : (t + 1) * 128]
        dq[t, 2] = dvt[:, t * 128 : (t + 1) * 128]
    wg[...] = jnp.zeros_like(wg)
    for s in range(3):
        r = dot(z[s * 96 : (s + 1) * 96], xf[...].reshape(1024, 768))
        for te in range(8):
            part = r[:, te * 96 : (te + 1) * 96].astype(BF)
            for j in range(4):
                wg[j % 2, 2 * te + j // 2, s, :, 0:96] = part[j * 24 : (j + 1) * 24]
    for c in range(32):
        wg[c % 2, c // 2, 3, :, 0:96] = go[c * 24 : (c + 1) * 24].astype(BF)


def backward(xf, q, k, v, pt, dr, att, wo):
    args = (xf, q, k, v, pt, dr, att, wo)
    return pl.pallas_call(
        backward_kernel,
        out_shape=[
            jax.ShapeDtypeStruct((8, 3, 96, 128), BF),
            jax.ShapeDtypeStruct((16, 2, 8, 32, 128), BF),
            jax.ShapeDtypeStruct((2, 16, 4, 24, 128), BF),
        ],
        in_specs=[VM] * len(args),
        out_specs=[VM] * 3,
        scratch_shapes=[
            pltpu.VMEM((128, 1024), BF),
            pltpu.VMEM((1024, 128), F32),
            pltpu.VMEM((1024, 128), F32),
            pltpu.VMEM((768, 96), F32),
            pltpu.VMEM((288, 1024), BF),
        ],
        compiler_params=pltpu.CompilerParams(vmem_limit_bytes=48 << 20),
    )(*args)


def layer_forward(values, scales):
    average = jnp.mean(values, axis=-1, keepdims=True)
    centred = values - average
    inverse = lax.rsqrt(jnp.mean(centred * centred, axis=-1, keepdims=True) + epsilon)
    normed = centred * inverse
    return (normed * scales, normed, inverse)


def layer_backward(upstream, scales, normed, inverse):
    scaled = upstream * scales
    first_moment = jnp.mean(scaled, axis=-1, keepdims=True)
    second_moment = jnp.mean(scaled * normed, axis=-1, keepdims=True)
    return inverse * (scaled - first_moment - normed * second_moment)


def per_device(
    noisy,
    single,
    pair,
    restype,
    chain,
    keymask,
    restype_table,
    norm_gain,
    pair_gain,
    trans_gain,
    w_query,
    w_key,
    w_value,
    w_out,
    w_pair,
    chain_weight,
    w_hidden_gate,
    w_hidden_up,
    w_down,
    cotangent,
):
    head = lax.axis_index(TOK)
    res_onehot = (restype[:, None] == jnp.arange(32, dtype=jnp.int32)[None, :]).astype(BF)
    condition = single.astype(F32) + dot(res_onehot, restype_table)
    noisy_f = noisy[0].astype(F32)
    normed_scaled, noisy_hat, noisy_inverse = layer_forward(noisy_f, norm_gain)
    x = (normed_scaled + condition).astype(BF)
    pair_t = jnp.transpose(pair, (1, 0, 2))
    pair_scaled, pair_hat, pair_inverse = layer_forward(pair_t.astype(F32), pair_gain)
    pair_rounded = pair_scaled.astype(BF)
    bias = jnp.einsum("jic,ch->hji", pair_rounded, w_pair, preferred_element_type=F32).astype(BF)
    xf, f = spread(x, bias)

    own_weight = lax.dynamic_slice_in_dim(chain_weight, head, 1, 1)
    key_weight = jnp.zeros((1024, 1), F32)
    for c in range(6):
        key_weight = jnp.where(chain[:, None] == c, own_weight[c : c + 1], key_weight)
    valid = (keymask > 0)[:, None]
    same = jnp.where(valid, key_weight, -1e30)
    diff = jnp.where(valid, jnp.zeros((1024, 1), F32), -1e30)
    att, pt, q, k, v = forward(
        xf, w_query, w_key, w_value, f, same, diff, chain[:, None], chain.reshape(8, 1, 128)
    )
    attended = exchange(att).reshape(768, 128)

    residual = noisy_f + dot(attended, w_out, 0, 0)
    trans_scaled, trans_hat, trans_inverse = layer_forward(residual, trans_gain)
    trans_in = trans_scaled.astype(BF)
    gate = dot(trans_in, w_hidden_gate)
    up_part = dot(trans_in, w_hidden_up)
    sigmoid_gate = jax.nn.sigmoid(gate)
    upstream = cotangent[0]
    d_hidden = dot(upstream, w_down, 1, 1)
    d_gate = (d_hidden * up_part * sigmoid_gate * (1.0 + gate * (1.0 - sigmoid_gate))).astype(BF)
    d_up = (d_hidden * gate * sigmoid_gate).astype(BF)
    d_trans = dot(d_gate, w_hidden_gate, 1, 1) + dot(d_up, w_hidden_up, 1, 1)
    d_res = upstream.astype(F32) + layer_backward(d_trans, trans_gain, trans_hat, trans_inverse)
    dr = gather(d_res.T.astype(BF))

    wo = jnp.pad(lax.dynamic_slice_in_dim(w_out, head * 96, 96, 0), ((0, 32), (0, 0)))
    dq, db, wg = backward(xf, q, k, v, pt, dr, att, wo)
    odq, odb, owg = home(dq, db, wg)

    odq = odq.reshape(3, 768, 128)
    d_in_t = dot(w_query, odq[0]) + dot(w_key, odq[1]) + dot(w_value, odq[2])
    grad_noisy = (d_res + layer_backward(d_in_t.T, norm_gain, noisy_hat, noisy_inverse)).astype(BF)
    gs = jnp.transpose(d_in_t.astype(BF).reshape(16, 2, 24, 128), (1, 0, 2, 3))
    d_pair_scaled = jnp.einsum("hji,ch->jic", odb, w_pair, preferred_element_type=F32)
    grad_pair = layer_backward(d_pair_scaled, pair_gain, pair_hat, pair_inverse).astype(BF)
    pw = jnp.einsum("hji,jic->hc", odb, pair_rounded, preferred_element_type=F32)
    ogs, opw = finish(gs, pw)
    grads = jnp.transpose(owg[:, :, :96].astype(F32), (0, 2, 1))
    return (
        grad_noisy[None],
        ogs.T,
        jnp.transpose(grad_pair, (1, 0, 2)),
        grads[0],
        grads[1],
        grads[2],
        grads[3],
        opw.T,
    )


def solution(mesh):
    torus = Mesh(
        mesh.devices.reshape(4, 4, 2, 2, 4), ("copy_0", "copy_1", "copy_2", "tok_0", "tok_1")
    )
    return jax.shard_map(
        per_device,
        mesh=torus,
        in_specs=(
            P(COPY, TOK, None),
            P(TOK, None),
            P(TOK, COPY, None),
            P(TOK),
            P(),
            P(),
            P(),
            P(),
            P(),
            P(),
            P(),
            P(),
            P(),
            P(),
            P(),
            P(),
            P(),
            P(),
            P(),
            P(COPY, TOK, None),
        ),
        out_specs=(
            P(COPY, TOK, None),
            P(TOK, COPY),
            P(TOK, COPY, None),
            P(TOK, COPY),
            P(TOK, COPY),
            P(TOK, COPY),
            P(TOK, COPY),
            P(),
        ),
        check_vma=False,
    )
```

time: 460 us -> 245 us (0.53)
  waiting for transfers between devices: 212 us -> 0 us
  Pallas kernels: 0 us -> 182 us
  blocking collectives: 62.2 us -> 0 us
  matrix products: 57.8 us -> 18.4 us
  starting transfers between devices: 31.6 us -> 0 us
  local copies, waits for them, and re-layouts: 48.1 us -> 28.8 us
  other arithmetic: 29.9 us -> 12 us
  between operations: 14.7 us -> 1.38 us
    pallas_call x0 -> x7, Pallas kernels: none -> 182 us  [the longest x5 158 us: comm_call(): pl.pallas_call(kernel, out_shape=outs, in_specs=[VM] * len(args), out_spe...]
    all_to_all x5 -> x0, waiting for transfers between devices: 89.2 us -> none  [the longest x2 64.5 us: summed_rows(): lax.all_to_all(own.astype(jnp.bfloat16), far, 0, 0, tiled=True)]
    unnamed x3 -> x0, waiting for transfers between devices: 80.9 us -> none
    all_gather x1 -> x0, waiting for transfers between devices: 42.2 us -> none  [sent_together(): filled, at, done = (lax.all_gather(both, axis, axis=dim, tiled=True), 0, [])]
    psum x5 -> x0, blocking collectives: 41.9 us -> none  [by_axis(): return functools.reduce(lax.psum, axes, shard)]
    dot_general x27 -> x12, matrix products: 57.8 us -> 18.4 us  [the longest x9 14.8 us: dot(): lax.dot_general(a, b, (((ca,), (cb,)), ((), ())), preferred_element_type=...]
    all_to_all x5 -> x0, starting transfers between devices: 31.5 us -> none  [the longest x2 11.4 us: summed_on_arrival(): lax.all_to_all(blocks, axis, split_axis=0, concat_axis=0, tiled=True)]
    all_to_all x3 -> x0, blocking collectives: 20.3 us -> none  [the longest x2 14.9 us: summed_on_arrival(): lax.all_to_all(blocks, axis, split_axis=0, concat_axis=0, tiled=True)]
  transfers between devices with their start and end apart: 7 -> 0, of which waited for: 5 -> 0; matrix products, arithmetic and copies ran while one was open for 15% -> 0% of each run, Pallas kernels for 0% -> 0%
where the time goes in v1:
time: 245 us; the launch traced here: 242 us
  Pallas kernels  182 us (74%)
  local copies, waits for them, and re-layouts  28.8 us (12%)
  matrix products  18.4 us (8%)
  other arithmetic  12 us (5%)
    pallas_call x5, Pallas kernels, comm_call(): pl.pallas_call(kernel, out_shape=outs, in_specs=[VM] * len(args), out_spe...  158 us
    unnamed x130, local copies, waits for them, and re-layouts  21.1 us
    dot_general x9, matrix products, dot(): lax.dot_general(a, b, (((ca,), (cb,)), ((), ())), preferred_element_type=...  14.8 us
    pallas_call x1, Pallas kernels, forward(): pl.pallas_call(forward_kernel, out_shape=[jax.ShapeDtypeStruct((8, 96, 12...  12 us
    pallas_call x1, Pallas kernels, backward(): pl.pallas_call(backward_kernel, out_shape=[jax.ShapeDtypeStruct((8, 3, 96...  11.9 us

profile of v1, /device:TPU:24, one launch (start us, length us, event | category | flops | bytes accessed | tf_op | source)
XLA Modules:
  0.0 242.1 jit_solution(15043843852698931715)
XLA Ops:
  0.7 0.9 constant_dynamic-slice_fusion.1
  1.6 0.5 fusion.59
  2.1 0.7 broadcast_select_fusion
  2.8 4.6 %select_select_fusion = f32[1024]{0:T(1024)S(1)} fusion(pred[1024]{0:T(1024)(128)(4,1)S(1)} %get-tuple-element.61, s32[1024]{0:T(1024)} %param.24, f32[]{:T(128)} %bitcast.10, f32[]{:T(128)} %bitcast.9, f32[]{:T(128)} %bitcast.8, f32[]{:T(128)} %bitcast.7, f32[]{:T(128)} %bitcast.6, f32[]{:T(128)} %bitcast.5), kind=kLoop, calls=%fused_computation.81 | loop fusion | flops 13312 | bytes 9240 | tf_op jit(solution)/shard_map/jit(_where)/select_n | solution.py:636
  7.4 0.9 constant_dynamic-slice_fusion
  8.3 0.7 pad.4.wo
  9.0 1.1 copy.48
  10.4 1.7 copy.47
  12.2 1.1 copy.49
  13.6 0.8 copy.54.x
  14.4 1.0 copy.55.same
  15.4 1.1 copy.56.diff
  16.5 1.0 copy.57.chj
  17.6 3.5 %fusion.39 = f32[128,1536]{1,0:T(8,128)} fusion(bf16[1536,768]{1,0:T(8,128)(2,1)} %param.38, bf16[1,128,768]{2,1,0:T(8,128)(2,1)S(1)} %copy-done.36), kind=kOutput, calls=%fused_computation.60 | convolution fusion | flops 301989888 | bytes 3342336 | tf_op jit(solution)/shard_map/dot_general | solution.py:19
  21.0 2.0 copy.51
  23.0 1.0 copy-done.26
  24.2 0.6 fusion.53
  24.8 2.0 fusion.11
  26.8 0.6 fusion.54
  27.5 0.6 copy-done.43
  28.0 1.7 fusion.42
  29.7 53.4 %shard_map.251 = (bf16[8,128,768]{2,1,0:T(8,128)(2,1)S(1)}, bf16[32,8,32,128]{3,2,1,0:T(8,128)(2,1)S(1)}) custom-call(bf16[128,768]{1,0:T(8,128)(2,1)S(1)} %copy-done.16, bf16[8,32,128]{2,1,0:T(8,128)(2,1)S(1)} %bitcast.139), custom_call_target="tpu_custom_call" | custom-call | tf_op jit(solution)/shard_map/pallas_call | solution.py:167
  83.2 1.2 copy-done.1
  84.4 1.3 copy-done.9
  85.7 1.0 copy-done.12
  86.8 12.0 %shard_map.252 = (bf16[8,96,128]{2,1,0:T(8,128)(2,1)S(1)}, bf16[8,1024,128]{2,1,0:T(8,128)(2,1)}, bf16[1024,128]{1,0:T(8,128)(2,1)S(1)}, bf16[1024,128]{1,0:T(8,128)(2,1)S(1)}, bf16[1024,128]{1,0:T(8,128)(2,1)S(1)}) custom-call(bf16[8,128,768]{2,1,0:T(8,128)(2,1)} %copy-done.1, bf16[768,768]{1,0:T(8,128)(2,1)S(1)} %copy-done.3, ...), custom_call_target="tpu_custom_call" | custom-call | tf_op jit(solution)/shard_map/pallas_call | solution.py:493
  98.8 0.7 copy-done.19
  99.5 0.7 copy-done.21
  100.2 10.6 %shard_map.253 = bf16[8,96,128]{2,1,0:T(8,128)(2,1)S(1)} custom-call(bf16[8,96,128]{2,1,0:T(8,128)(2,1)S(1)} %get-tuple-element.25.a.att), custom_call_target="tpu_custom_call" | custom-call | tf_op jit(solution)/shard_map/pallas_call | solution.py:167
  110.8 0.7 copy-done.13
  111.5 0.6 fusion.60
  112.2 0.6 copy-done.29
  112.8 1.5 fusion.55
  114.3 4.3 %fusion.19 = f32[128,768]{0,1:T(8,128)} fusion(bf16[768,1536]{1,0:T(8,128)(2,1)S(1)} %copy-done, f32[128,1536]{1,0:T(8,128)} %fusion.39, bf16[768,1536]{1,0:T(8,128)(2,1)} %param.37, f32[128,1536]{1,0:T(8,128)} %fusion.55, f32[128,768]{0,1:T(8,128)} %copy-done.29, f32[768]{0:T(1024)S(1)} %copy-done.52, f32[128]{0:T(128)S(1)} %add_rsqrt_fusion.1, ...), kind=kOutput, calls=%fused_computation.29 | convolution fusion | flops 606339072 | bytes 7081984 | tf_op jit(solution)/shard_map/dot_general | solution.py:19
  118.6 3.2 %fusion.56 = (f32[128]{0:T(128)S(1)}, f32[128]{0:T(128)S(1)}, f32[128,768]{0,1:T(8,128)S(1)}) fusion(f32[128]{0:T(128)S(1)} %add_rsqrt_fusion.1, f32[128,768]{0,1:T(8,128)} %copy-done.29, f32[128]{0:T(128)S(1)} %broadcast_multiply_fusion.5, f32[768]{0:T(1024)S(1)} %copy-done.52, f32[128,768]{0,1:T(8,128)} %fusion.19, bf16[768,1536]{1,0:T(8,128)(2,1)} %param.37, ...), kind=kOutput, calls=%fused_computation.101 | convolution fusion | flops 303857408 | bytes 5116928 | tf_op jit(solution)/shard_map/dot_general | solution.py:19
  122.1 19.5 %shard_map.254.dr = bf16[8,768,128]{2,1,0:T(8,128)(2,1)S(1)} custom-call(bf16[768,128]{1,0:T(8,128)(2,1)S(1)} %convert_bitcast_fusion.2.a), custom_call_target="tpu_custom_call" | custom-call | tf_op jit(solution)/shard_map/pallas_call | solution.py:167
  141.6 11.9 %shard_map.255 = (bf16[8,3,96,128]{3,2,1,0:T(8,128)(2,1)S(1)}, bf16[16,2,8,32,128]{4,3,2,1,0:T(8,128)(2,1)}, bf16[2,16,4,24,128]{4,3,2,1,0:T(8,128)(2,1)S(1)}) custom-call(bf16[8,128,768]{2,1,0:T(8,128)(2,1)S(1)} %copy-done.2, bf16[1024,128]{1,0:T(8,128)(2,1)S(1)} %copy-done.18, bf16[1024,128]{1,0:T(8,128)(2,1)S(1)} %copy-done.20, ...), custom_call_target="tpu_custom_call" | custom-call | tf_op jit(solution)/shard_map/pallas_call | solution.py:562
  153.5 1.6 copy-done.8
  155.1 50.7 %shard_map.256 = (bf16[3,8,96,128]{3,2,1,0:T(8,128)(2,1)S(1)}, bf16[8,32,128]{2,1,0:T(8,128)(2,1)S(1)}, bf16[4,24,128]{2,1,0:T(8,128)(2,1)S(1)}) custom-call(bf16[8,3,96,128]{3,2,1,0:T(8,128)(2,1)S(1)} %get-tuple-element.30.dq, bf16[16,2,8,32,128]{4,3,2,1,0:T(8,128)(2,1)S(1)} %copy-done.8, bf16[2,16,4,24,128]{4,3,2,1,0:T(8,128)(2,1)S(1)} %get-tuple-element.32.wg), custom_call_target="tpu_custom_call" | custom-call | tf_op jit(solution)/shard_map/pallas_call | solution.py:167
  206.4 0.6 slice_bitcast_fusion
  208.6 0.9 fusion.58
  209.6 23.6 %shard_map.257 = (f32[24,128]{1,0:T(8,128)S(1)}, f32[8,128]{1,0:T(8,128)S(1)}) custom-call(bf16[2,16,24,128]{3,2,1,0:T(8,128)(2,1)S(1)} %bitcast.138, f32[8,128]{1,0:T(8,128)S(1)} %convolution_bitcast_fusion.pw), custom_call_target="tpu_custom_call" | custom-call | tf_op jit(solution)/shard_map/pallas_call | solution.py:167
  233.2 1.7 copy.68
  235.0 1.4 multiply_reduce_fusion
  236.5 1.8 fusion.16
  238.3 2.6 %copy.69 = bf16[128,32,128]{2,1,0:T(8,128)(2,1)} copy(bf16[128,32,128]{0,2,1:T(8,128)(2,1)} %fusion.16) | data formatting | bytes 2097152
  240.9 0.6 copy.93
  241.5 0.6 copy.94
  (135 shorter events, 3.3 us)
Async XLA Ops:
  0.6 112.2 %copy-start = (bf16[768,1536]{1,0:T(8,128)(2,1)S(1)}, bf16[768,1536]{1,0:T(8,128)(2,1)}, u32[]{:S(2)}) copy-start(bf16[768,1536]{1,0:T(8,128)(2,1)} %param.36) | copy-start | bytes 7077892
  0.6 12.6 %copy-start.41 = (f32[768]{0:T(1024)S(1)}, f32[768]{0:T(1024)}, u32[]{:S(2)}) copy-start(f32[768]{0:T(1024)} %param.27) | copy-start | bytes 9220
  0.7 12.6 %copy-start.58 = (bf16[32,768]{1,0:T(8,128)(2,1)S(1)}, bf16[32,768]{1,0:T(8,128)(2,1)}, u32[]{:S(2)}) copy-start(bf16[32,768]{1,0:T(8,128)(2,1)} %param.26) | copy-start | bytes 147460
  0.7 12.6 %copy-start.60 = (s32[128]{0:T(128)S(1)}, s32[128]{0:T(128)}, u32[]{:S(2)}) copy-start(s32[128]{0:T(128)} %param.23) | copy-start | bytes 1540
  8.3 8.2 %copy-start.23 = (s32[1024]{0:T(1024)S(1)}, s32[1024]{0:T(1024)}, u32[]{:S(2)}) copy-start(s32[1024]{0:T(1024)} %param.24) | copy-start | bytes 12292
  9.0 8.5 %copy-start.36 = (bf16[1,128,768]{2,1,0:T(8,128)(2,1)S(1)}, bf16[1,128,768]{2,1,0:T(8,128)(2,1)}, u32[]{:S(2)}) copy-start(bf16[1,128,768]{2,1,0:T(8,128)(2,1)} %param.39) | copy-start | bytes 589828
  10.2 7.4 %copy-start.31 = (bf16[1,128,768]{1,2,0:T(8,128)(2,1)}, bf16[1,128,768]{1,2,0:T(8,128)(2,1)S(1)}, u32[]{:S(2)}) copy-start(bf16[1,128,768]{1,2,0:T(8,128)(2,1)S(1)} %copy.48) | copy-start | bytes 589828
  10.3 7.3 %copy-start.50 = (f32[128]{0:T(128)}, f32[128]{0:T(128)S(1)}, u32[]{:S(2)}) copy-start(f32[128]{0:T(128)S(1)} %broadcast_multiply_fusion.6) | copy-start | bytes 1540
  10.4 7.1 %copy-start.53 = (f32[128]{0:T(128)}, f32[128]{0:T(128)S(1)}, u32[]{:S(2)}) copy-start(f32[128]{0:T(128)S(1)} %add_rsqrt_fusion.2) | copy-start | bytes 1540
  21.0 7.0 %copy-start.55 = (f32[128]{0:T(128)S(1)}, f32[128]{0:T(128)}, u32[]{:S(2)}) copy-start(f32[128]{0:T(128)} %param.28) | copy-start | bytes 1540
  21.0 7.0 %copy-start.59 = (bf16[128,8]{0,1:T(8,128)(2,1)S(1)}, bf16[128,8]{0,1:T(8,128)(2,1)}, u32[]{:S(2)}) copy-start(bf16[128,8]{0,1:T(8,128)(2,1)} %param.34) | copy-start | bytes 6148
  24.0 5.7 %copy-start.16 = (bf16[128,768]{1,0:T(8,128)(2,1)S(1)}, bf16[128,768]{1,0:T(8,128)(2,1)}, u32[]{:S(2)}) copy-start(bf16[128,768]{1,0:T(8,128)(2,1)} %copy.54.x) | copy-start | bytes 589828
  24.0 61.7 %copy-start.10 = (f32[1024,1]{1,0:T(8,128)S(1)}, f32[1024,1]{1,0:T(8,128)}, u32[]{:S(2)}) copy-start(f32[1024,1]{1,0:T(8,128)} %copy.55.same) | copy-start | bytes 12292
  24.0 61.7 %copy-start.11 = (f32[1024,1]{1,0:T(8,128)S(1)}, f32[1024,1]{1,0:T(8,128)}, u32[]{:S(2)}) copy-start(f32[1024,1]{1,0:T(8,128)} %copy.56.diff) | copy-start | bytes 12292
  24.2 61.5 %copy-start.3 = (bf16[768,768]{1,0:T(8,128)(2,1)S(1)}, bf16[768,768]{1,0:T(8,128)(2,1)}, u32[]{:S(2)}) copy-start(bf16[768,768]{1,0:T(8,128)(2,1)} %wq.1) | copy-start | bytes 3538948
  24.2 61.5 %copy-start.4 = (bf16[768,768]{1,0:T(8,128)(2,1)S(1)}, bf16[768,768]{1,0:T(8,128)(2,1)}, u32[]{:S(2)}) copy-start(bf16[768,768]{1,0:T(8,128)(2,1)} %wk.1) | copy-start | bytes 3538948
  24.2 61.5 %copy-start.6 = (bf16[768,768]{1,0:T(8,128)(2,1)S(1)}, bf16[768,768]{1,0:T(8,128)(2,1)}, u32[]{:S(2)}) copy-start(bf16[768,768]{1,0:T(8,128)(2,1)} %wv.1) | copy-start | bytes 3538948
  24.8 2.6 %copy-start.39 = (f32[32,128]{1,0:T(8,128)}, f32[32,128]{1,0:T(8,128)S(1)}, u32[]{:S(2)}) copy-start(f32[32,128]{1,0:T(8,128)S(1)} %get-tuple-element.74) | copy-start | bytes 49156
  86.8 24.7 %copy-start.32 = (bf16[1,128,768]{1,2,0:T(8,128)(2,1)S(1)}, bf16[1,128,768]{1,2,0:T(8,128)(2,1)}, u32[]{:S(2)}) copy-start(bf16[1,128,768]{1,2,0:T(8,128)(2,1)} %copy-done.31) | copy-start | bytes 589828
  86.8 24.7 %copy-start.35 = (bf16[768,768]{1,0:T(8,128)(2,1)S(1)}, bf16[768,768]{1,0:T(8,128)(2,1)}, u32[]{:S(2)}) copy-start(bf16[768,768]{1,0:T(8,128)(2,1)} %param.33) | copy-start | bytes 3538948
  100.2 11.8 %copy-start.17 = (bf16[1024,128]{1,0:T(8,128)(2,1)}, bf16[1024,128]{1,0:T(8,128)(2,1)S(1)}, u32[]{:S(2)}) copy-start(bf16[1024,128]{1,0:T(8,128)(2,1)S(1)} %get-tuple-element.26.q) | copy-start | bytes 786436
  100.2 12.6 %copy-start.52 = (f32[768]{0:T(1024)S(1)}, f32[768]{0:T(1024)}, u32[]{:S(2)}) copy-start(f32[768]{0:T(1024)} %param.29) | copy-start | bytes 9220
  112.1 9.8 %copy-start.46 = (f32[128]{0:T(128)}, f32[128]{0:T(128)S(1)}, u32[]{:S(2)}) copy-start(f32[128]{0:T(128)S(1)} %broadcast_multiply_fusion.5) | copy-start | bytes 1540
  112.8 9.1 %copy-start.48 = (f32[128]{0:T(128)}, f32[128]{0:T(128)S(1)}, u32[]{:S(2)}) copy-start(f32[128]{0:T(128)S(1)} %add_rsqrt_fusion.1) | copy-start | bytes 1540
  118.6 3.3 %copy-start.30 = (f32[128,768]{0,1:T(8,128)S(1)}, f32[128,768]{0,1:T(8,128)}, u32[]{:S(2)}) copy-start(f32[128,768]{0,1:T(8,128)} %copy-done.29) | copy-start | bytes 1179652
  118.6 3.3 %copy-start.34 = (bf16[1,128,768]{1,2,0:T(8,128)(2,1)S(1)}, bf16[1,128,768]{1,2,0:T(8,128)(2,1)}, u32[]{:S(2)}) copy-start(bf16[1,128,768]{1,2,0:T(8,128)(2,1)} %copy.47) | copy-start | bytes 589828
  121.8 19.7 %copy-start.2 = (bf16[8,128,768]{2,1,0:T(8,128)(2,1)S(1)}, bf16[8,128,768]{2,1,0:T(8,128)(2,1)}, u32[]{:S(2)}) copy-start(bf16[8,128,768]{2,1,0:T(8,128)(2,1)} %copy-done.1) | copy-start | bytes 4718596
  121.8 19.7 %copy-start.14 = (bf16[8,96,128]{2,1,0:T(8,128)(2,1)S(1)}, bf16[8,96,128]{2,1,0:T(8,128)(2,1)}, u32[]{:S(2)}) copy-start(bf16[8,96,128]{2,1,0:T(8,128)(2,1)} %copy-done.13) | copy-start | bytes 589828
  121.8 19.7 %copy-start.15 = (bf16[128,768]{1,0:T(8,128)(2,1)S(1)}, bf16[128,768]{1,0:T(8,128)(2,1)}, u32[]{:S(2)}) copy-start(bf16[128,768]{1,0:T(8,128)(2,1)} %pad.4.wo) | copy-start | bytes 589828
  121.8 19.7 %copy-start.18 = (bf16[1024,128]{1,0:T(8,128)(2,1)S(1)}, bf16[1024,128]{1,0:T(8,128)(2,1)}, u32[]{:S(2)}) copy-start(bf16[1024,128]{1,0:T(8,128)(2,1)} %copy-done.17) | copy-start | bytes 786436
  121.8 19.7 %copy-start.20 = (bf16[1024,128]{1,0:T(8,128)(2,1)S(1)}, bf16[1024,128]{1,0:T(8,128)(2,1)}, u32[]{:S(2)}) copy-start(bf16[1024,128]{1,0:T(8,128)(2,1)} %copy-done.19) | copy-start | bytes 786436
  121.9 19.7 %copy-start.22 = (bf16[1024,128]{1,0:T(8,128)(2,1)S(1)}, bf16[1024,128]{1,0:T(8,128)(2,1)}, u32[]{:S(2)}) copy-start(bf16[1024,128]{1,0:T(8,128)(2,1)} %copy-done.21) | copy-start | bytes 786436
  155.1 50.8 %copy-start.27 = (bf16[128,32,128]{0,2,1:T(8,128)(2,1)S(1)}, bf16[128,32,128]{0,2,1:T(8,128)(2,1)}, u32[]{:S(2)}) copy-start(bf16[128,32,128]{0,2,1:T(8,128)(2,1)} %copy-done.26) | copy-start | bytes 3145732
  155.1 50.8 %copy-start.40 = (f32[32,128]{1,0:T(8,128)S(1)}, f32[32,128]{1,0:T(8,128)}, u32[]{:S(2)}) copy-start(f32[32,128]{1,0:T(8,128)} %copy-done.39) | copy-start | bytes 49156
  155.1 50.8 %copy-start.44 = (f32[32,128]{1,0:T(8,128)S(1)}, f32[32,128]{1,0:T(8,128)}, u32[]{:S(2)}) copy-start(f32[32,128]{1,0:T(8,128)} %copy-done.43) | copy-start | bytes 49156
  155.1 50.8 %copy-start.56 = (f32[128]{0:T(128)S(1)}, f32[128]{0:T(128)}, u32[]{:S(2)}) copy-start(f32[128]{0:T(128)} %param.28) | copy-start | bytes 1540
  205.7 1.7 copy-start.24
  205.8 1.7 copy-start.5
  206.3 1.7 copy-start.7
  206.3 1.7 copy-start.33
  206.3 1.7 copy-start.42
  206.3 1.7 copy-start.51
  206.3 1.7 copy-start.54
  208.1 26.9 %copy-start.25 = (bf16[8,32,128]{2,1,0:T(8,128)(2,1)S(1)}, bf16[8,32,128]{2,1,0:T(8,128)(2,1)}, u32[]{:S(2)}) copy-start(bf16[8,32,128]{2,1,0:T(8,128)(2,1)} %copy-done.24) | copy-start | bytes 196612
  208.1 26.9 %copy-start.28 = (bf16[128,32,128]{0,2,1:T(8,128)(2,1)S(1)}, bf16[128,32,128]{0,2,1:T(8,128)(2,1)}, u32[]{:S(2)}) copy-start(bf16[128,32,128]{0,2,1:T(8,128)(2,1)} %copy-done.26) | copy-start | bytes 3145732
  208.1 26.9 %copy-start.45 = (f32[32,128]{1,0:T(8,128)S(1)}, f32[32,128]{1,0:T(8,128)}, u32[]{:S(2)}) copy-start(f32[32,128]{1,0:T(8,128)} %copy-done.43) | copy-start | bytes 49156
  209.6 26.9 %copy-start.37 = (f32[128,32]{0,1:T(8,128)S(1)}, f32[128,32]{0,1:T(8,128)}, u32[]{:S(2)}) copy-start(f32[128,32]{0,1:T(8,128)} %get-tuple-element.73) | copy-start | bytes 49156
  209.6 26.9 %copy-start.38 = (f32[128,32]{0,1:T(8,128)S(1)}, f32[128,32]{0,1:T(8,128)}, u32[]{:S(2)}) copy-start(f32[128,32]{0,1:T(8,128)} %get-tuple-element.71) | copy-start | bytes 49156
  (13 other events, 13.3 us)

commit v2 on v0

v2 whole, which is shorter than its diff:
```python
import jax
import jax.numpy as jnp
from jax import lax
from jax.experimental import pallas as pl
from jax.experimental.pallas import tpu as pltpu
from jax.sharding import Mesh
from jax.sharding import PartitionSpec as P

TOK = ("tok_0", "tok_1")
COPY = ("copy_0", "copy_1", "copy_2")
MESH = pl.DeviceIdType.MESH
VM = pl.BlockSpec(memory_space=pltpu.VMEM)
BF = jnp.bfloat16
F32 = jnp.float32
epsilon = 1e-05


def dot(a, b, ca=1, cb=0):
    return lax.dot_general(a, b, (((ca,), (cb,)), ((), ())), preferred_element_type=F32)


class Place:
    def __init__(self):
        self.y = lax.axis_index("copy_0")
        self.z = lax.axis_index("copy_1")
        self.core = lax.axis_index("copy_2")
        self.zh = lax.axis_index("tok_0")
        self.x = lax.axis_index("tok_1")
        self.tok = self.zh * 4 + self.x
        self.chip = self.y * 4 + self.z
        self.copy = self.chip * 2 + self.core

    def around_y(self, d):
        return {"copy_0": lax.rem(self.y + d, 4)}

    def around_z(self, d):
        return {"copy_1": lax.rem(self.z + d, 4)}

    def around_x(self, d):
        return {"tok_1": lax.rem(self.x + d, 4)}

    def other_core(self):
        return {"copy_2": 1 - self.core}

    def other_half(self):
        return {"tok_0": 1 - self.zh}

    def tok_at(self, d):
        t = lax.rem(self.tok + d, 8)
        return t, {"tok_0": t // 4, "tok_1": lax.rem(t, 4)}


class Wire:
    def __init__(self, send, recv):
        self.send, self.recv, self.at, self.open = send, recv, 0, []

    def take(self, n):
        k = self.at
        self.at += n
        return k

    def copy(self, src, dst, device, k):
        return pltpu.make_async_remote_copy(
            src_ref=src,
            dst_ref=dst,
            send_sem=self.send.at[k],
            recv_sem=self.recv.at[k],
            device_id=device,
            device_id_type=MESH,
        )

    def go(self, src, dst, device):
        c = self.copy(src, dst, device, self.take(1))
        c.start()
        self.open.append(c)
        return c

    def close(self):
        for c in self.open:
            c.wait_send()


def turns(*chains):
    chains = list(chains)
    while chains:
        for c in list(chains):
            if next(c, 0) == 0:
                chains.remove(c)


def step(chain, n=1):
    for _ in range(n):
        next(chain, 0)


def gather_chain(w, me, src, out, rows):
    half = rows // 2
    lo = lax.rem(me.x + 3, 4)
    hi = lax.rem(me.x + 1, 4)
    far = w.go(src, out.at[me.tok], me.other_half())
    left = w.go(src, out.at[me.tok], me.around_x(3))
    right = w.go(src, out.at[me.tok], me.around_x(1))
    tail = []

    def ring_pass(left, right, zh):
        right.wait_recv()
        r = out.at[zh * 4 + lo, pl.ds(0, half)]
        tail.append(w.go(r, r, me.around_x(1)))
        left.wait_recv()
        r = out.at[zh * 4 + hi, pl.ds(half, half)]
        tail.append(w.go(r, r, me.around_x(3)))

    yield 1
    ring_pass(left, right, me.zh)
    yield 1
    far.wait_recv()
    oz = 1 - me.zh
    r = out.at[oz * 4 + me.x]
    left = w.go(r, r, me.around_x(3))
    right = w.go(r, r, me.around_x(1))
    yield 1
    for c in tail:
        c.wait_recv()
    tail.clear()
    yield 1
    ring_pass(left, right, oz)
    yield 1
    for c in tail:
        c.wait_recv()


def bias_chain(w, me, bt, f, toks):
    heads = [w.go(bt.at[t], f.at[me.copy, me.tok], d) for t, d in toks]
    f[me.copy, me.tok] = bt[me.tok]
    mine = pl.ds(4 * me.core, 4)
    theirs = pl.ds(4 * (1 - me.core), 4)
    yield 1
    for h in heads:
        h.wait_recv()
    first = w.go(f.at[me.copy, theirs], f.at[me.copy, theirs], me.other_core())
    yield 1
    first.wait_recv()
    chip = f.at[pl.ds(me.chip * 2, 2), mine]
    zs = [w.go(chip, chip, me.around_z(k)) for k in (1, 2, 3)]
    last = [w.go(f.at[me.copy, mine], f.at[me.copy, mine], me.other_core())]
    yield 1
    for c in zs:
        c.wait_recv()
    row = f.at[pl.ds(me.y * 8, 8), mine]
    left = w.go(row, row, me.around_y(3))
    right = w.go(row, row, me.around_y(1))
    for k in (1, 2, 3):
        r = f.at[pl.ds((me.y * 4 + lax.rem(me.z + 4 - k, 4)) * 2, 2), mine]
        last.append(w.go(r, r, me.other_core()))
    lo = lax.rem(me.y + 3, 4) * 8
    hi = lax.rem(me.y + 1, 4) * 8
    op = lax.rem(me.y + 2, 4) * 8
    yield 1
    right.wait_recv()
    r = f.at[pl.ds(lo, 4), mine]
    a = w.go(r, r, me.around_y(1))
    r = f.at[pl.ds(lo, 8), mine]
    last.append(w.go(r, r, me.other_core()))
    left.wait_recv()
    r = f.at[pl.ds(hi + 4, 4), mine]
    b = w.go(r, r, me.around_y(3))
    r = f.at[pl.ds(hi, 8), mine]
    last.append(w.go(r, r, me.other_core()))
    yield 1
    a.wait_recv()
    r = f.at[pl.ds(op, 4), mine]
    last.append(w.go(r, r, me.other_core()))
    b.wait_recv()
    r = f.at[pl.ds(op + 4, 4), mine]
    last.append(w.go(r, r, me.other_core()))
    for c in last:
        c.wait_recv()


def add_into(dst, a, b):
    dst[...] = (a[...].astype(F32) + b[...].astype(F32)).astype(dst.dtype)


def scatter_chain(w, me, s, bufs, done):
    near_a, near_b, from_l, from_r, from_z = bufs
    opp = lax.rem(me.y + 2, 4) * 4
    lo = lax.rem(me.y + 3, 4) * 4
    hi = lax.rem(me.y + 1, 4) * 4
    a = w.go(s.at[pl.ds(opp, 2)], near_a, me.around_y(3))
    b = w.go(s.at[pl.ds(opp + 2, 2)], near_b, me.around_y(1))
    yield 1
    a.wait_recv()
    add_into(s.at[pl.ds(lo, 2)], s.at[pl.ds(lo, 2)], near_a)
    b.wait_recv()
    add_into(s.at[pl.ds(hi + 2, 2)], s.at[pl.ds(hi + 2, 2)], near_b)
    c = w.go(s.at[pl.ds(lo, 4)], from_r, me.around_y(3))
    d = w.go(s.at[pl.ds(hi, 4)], from_l, me.around_y(1))
    yield 1
    c.wait_recv()
    d.wait_recv()
    own = s.at[pl.ds(me.y * 4, 4)]
    own[...] = (
        own[...].astype(F32) + from_l[...].astype(F32) + from_r[...].astype(F32)
    ).astype(own.dtype)
    zs = []
    for k in (1, 2, 3):
        zt = lax.rem(me.z + k, 4)
        zs.append(w.go(s.at[me.y * 4 + zt], from_z.at[k - 1], me.around_z(k)))
    yield 1
    for k in zs:
        k.wait_recv()
    total = s[me.chip].astype(F32)
    for k in range(3):
        total = total + from_z[k].astype(F32)
    done(total)


def scatter_scratch(rest):
    return [
        pltpu.VMEM((2, *rest), BF),
        pltpu.VMEM((2, *rest), BF),
        pltpu.VMEM((4, *rest), BF),
        pltpu.VMEM((4, *rest), BF),
        pltpu.VMEM((3, *rest), BF),
    ]


def layer_forward(values, scales):
    average = jnp.mean(values, axis=-1, keepdims=True)
    centred = values - average
    inverse = lax.rsqrt(jnp.mean(centred * centred, axis=-1, keepdims=True) + epsilon)
    normed = centred * inverse
    return (normed * scales, normed, inverse)


def layer_backward(upstream, scales, normed, inverse):
    scaled = upstream * scales
    first_moment = jnp.mean(scaled, axis=-1, keepdims=True)
    second_moment = jnp.mean(scaled * normed, axis=-1, keepdims=True)
    return inverse * (scaled - first_moment - normed * second_moment)


INPUTS = (
    ("noisy", "single", "pair", "restype", "chain", "keymask", "table")
    + ("ng", "pg", "tg", "wp", "cot", "cw")
    + ("wq_h", "wk_h", "wv_h", "wo_h", "wg_h", "wu_h", "wd_h")
)
OUTPUTS = ("gn", "ogs", "gp", "owg", "opw")
OUT_SHAPES = (
    ((128, 768), BF),
    ((24, 128), F32),
    ((32, 128, 128), BF),
    ((4, 24, 128), BF),
    ((8, 128), F32),
)
V = pltpu.VMEM
SCRATCH = dict(
    wq=V((768, 768), BF),
    wk=V((768, 768), BF),
    wv=V((768, 768), BF),
    wo=V((768, 768), BF),
    wgate=V((768, 1536), BF),
    wup=V((768, 1536), BF),
    wdown=V((1536, 768), BF),
    load=pltpu.SemaphoreType.DMA((7,)),
    send=pltpu.SemaphoreType.DMA((140,)),
    recv=pltpu.SemaphoreType.DMA((140,)),
    xs=V((128, 768), BF),
    xf=V((8, 128, 768), BF),
    pr=V((32, 128, 128), BF),
    bj=V((256, 128), F32),
    bt=V((8, 32, 128), BF),
    f=V((32, 8, 32, 128), BF),
    ab=V((1024, 128), F32),
    bb=V((1024, 128), F32),
    cb=V((1024, 128), F32),
    q=V((1024, 128), BF),
    k=V((1024, 128), BF),
    v=V((1024, 128), BF),
    kt=V((128, 1024), BF),
    vt=V((128, 1024), BF),
    pt=V((8, 1024, 128), BF),
    att=V((8, 96, 128), BF),
    attl=V((8, 96, 128), BF),
    dh=V((128, 1536), F32),
    dres=V((128, 768), F32),
    drs=V((768, 128), BF),
    dr=V((8, 768, 128), BF),
    dq=V((8, 3, 96, 128), BF),
    odq=V((3, 8, 96, 128), BF),
    db=V((16, 2, 8, 32, 128), BF),
    dk=V((1024, 128), F32),
    dv=V((1024, 128), F32),
    go=V((768, 96), F32),
    zz=V((288, 1024), BF),
    wg=V((2, 16, 4, 24, 128), BF),
    wg1=V((16, 4, 24, 128), BF),
    ws=V((16, 4, 24, 128), BF),
    gt=V((4, 24, 128), BF),
    db1=V((16, 2, 4, 32, 128), BF),
    s1=V((16, 2, 4, 32, 128), BF),
    bu=V((2, 4, 32, 128), BF),
    bl=V((8, 32, 128), BF),
    odb=V((8, 32, 128), BF),
    gj=V((256, 128), F32),
    gs=V((2, 16, 24, 128), BF),
    gs1=V((16, 24, 128), BF),
    ss=V((16, 24, 128), BF),
    p0=V((8, 128), F32),
    p1=V((8, 128), F32),
    p2=V((8, 128), F32),
    p3=V((8, 128), F32),
    r0=V((8, 128), F32),
    r1=V((3, 8, 128), F32),
    r2=V((3, 8, 128), F32),
    r3=V((8, 8, 128), F32),
)
for name, rest in (("bw", (4, 24, 128)), ("bd", (2, 4, 32, 128)), ("bg", (24, 128))):
    for at, ref in enumerate(scatter_scratch(rest)):
        SCRATCH[name + str(at)] = ref


class Refs:
    pass


def block_kernel(*refs):
    r = Refs()
    for name, ref in zip(INPUTS + OUTPUTS + tuple(SCRATCH), refs):
        setattr(r, name, ref)
    me = Place()
    w = Wire(r.send, r.recv)
    h = me.tok
    scale = 96**-0.5
    toks = [me.tok_at(d) for d in range(1, 8)]
    turn = me.tok * 4 + lax.rem(me.copy, 4)
    turn_tok = me.copy // 4
    other = turn_tok != me.tok
    partner = {
        "copy_0": turn // 8,
        "copy_1": lax.rem(turn // 2, 4),
        "copy_2": lax.rem(turn, 2),
        "tok_0": turn_tok // 4,
        "tok_1": lax.rem(turn_tok, 4),
    }

    barrier = pltpu.get_barrier_semaphore()
    peers = [d for _, d in toks] + [me.other_core()]
    peers += [me.around_z(k) for k in (1, 2, 3)] + [me.around_y(k) for k in (1, 2, 3)]
    for d in peers:
        pl.semaphore_signal(barrier, inc=1, device_id=d, device_id_type=MESH)

    @pl.when(other)
    def _():
        pl.semaphore_signal(barrier, inc=1, device_id=partner, device_id_type=MESH)

    pairs = (
        (r.wq_h, r.wq),
        (r.wk_h, r.wk),
        (r.wv_h, r.wv),
        (r.wd_h, r.wdown),
        (r.wo_h, r.wo),
        (r.wg_h, r.wgate),
        (r.wu_h, r.wup),
    )
    loads = [pltpu.make_async_copy(a, b, r.load.at[n]) for n, (a, b) in enumerate(pairs)]
    for c in loads:
        c.start()

    noisy_f = r.noisy[...].astype(F32)
    classes = lax.broadcasted_iota(jnp.int32, (32, 128), 0) == r.restype[...]
    classes = jnp.where(classes, 1.0, 0.0).astype(BF)
    condition = r.single[...].astype(F32) + dot(classes, r.table[...], 0, 0)
    x = (layer_forward(noisy_f, r.ng[...])[0] + condition).astype(BF)
    r.xs[...] = x
    r.xf[me.tok] = x
    pl.semaphore_wait(barrier, len(peers) + jnp.where(other, 1, 0))
    xs = gather_chain(w, me, r.xs, r.xf, 128)
    step(xs)

    @pl.loop(0, 32)
    def _(j):
        p = layer_forward(r.pair[j].astype(F32), r.pg[...])[0].astype(BF)
        r.pr[j] = p
        r.bj[pl.ds(pl.multiple_of(j * 8, 8), 8)] = dot(r.wp[...], p, 1, 1)

    for n in range(8):
        r.bt[n] = r.bj[pl.ds(n, 32, stride=8)].astype(BF)
    bs = bias_chain(w, me, r.bt, r.f, toks)
    step(bs)
    step(xs)
    for t in range(8):
        code = jnp.where(r.keymask[t : t + 1] > 0, r.chain[t : t + 1], r.chain[t : t + 1] + 8)
        code = jnp.broadcast_to(code.astype(F32), (128, 128)).T
        rows = pl.ds(t * 128, 128)
        r.cb[rows] = code
        same = jnp.zeros((128, 128), F32)
        for c in range(6):
            same = jnp.where(code == c, r.cw[c, h], same)
        r.ab[rows] = same
        r.bb[rows] = jnp.where(code >= 8, -1e30, 0.0)
    step(bs)
    for c in loads[:3]:
        c.wait()
    row = lax.broadcasted_iota(jnp.int32, (768, 128), 0)
    col = lax.broadcasted_iota(jnp.int32, (768, 128), 1)
    pick = jnp.where((row == col + h * 96) & (col < 96), 1.0, 0.0).astype(BF)
    heads = [dot(m[...], pick).astype(BF) for m in (r.wq, r.wk, r.wv)]

    def project(t):
        rows = pl.ds(pl.multiple_of(t * 128, 128), 128)
        for m, o in zip(heads, (r.q, r.k, r.v)):
            o[rows] = dot(r.xf[t], m).astype(BF)

    step(bs)
    step(xs)
    loads[3].wait()
    r.dh[...] = dot(r.cot[...], r.wdown[...], 1, 1)
    step(xs)
    step(bs)
    for t in range(4):
        project(me.zh * 4 + t)
    step(xs)
    step(bs)
    step(xs)
    for t in range(4):
        project((1 - me.zh) * 4 + t)
    r.vt[...] = r.v[...].T
    r.kt[...] = r.k[...].T
    turns(bs, xs)

    ak = w.take(7)

    def att_copy(s, t):
        device = {"tok_0": t // 4, "tok_1": lax.rem(t, 4)}
        return w.copy(r.att.at[t], r.attl.at[me.tok], device, ak + s)

    @pl.loop(0, 8)
    def _(s):
        t = lax.rem(me.tok + 1 + s, 8)

        @pl.when(s > 0)
        def _():
            att_copy(s - 1, lax.rem(me.tok + s, 8)).start()

        rows = pl.ds(pl.multiple_of(t * 128, 128), 128)
        a = dot(r.k[...], r.q[rows], 1, 1)
        bias = r.f[:, t].reshape(1024, 128).astype(F32)
        own = r.chain[pl.ds(t, 1)].astype(F32)
        a = a * scale + (bias + jnp.where(r.cb[...] == own, r.ab[...], r.bb[...]))
        e = jnp.exp(a - jnp.max(a, axis=0, keepdims=True))
        p = (e * (1.0 / jnp.sum(e, axis=0, keepdims=True))).astype(BF)
        r.pt[t] = p
        r.att[t] = dot(r.vt[...], p)[:96].astype(BF)

    r.attl[me.tok] = r.att[me.tok]
    for s in range(7):
        att_copy(s, toks[s][0]).wait()

    for c in loads[4:]:
        c.wait()
    residual = noisy_f + dot(r.attl[...].reshape(768, 128), r.wo[...], 0, 0)
    scaled, trans_hat, trans_inverse = layer_forward(residual, r.tg[...])
    trans_in = scaled.astype(BF)
    d_trans = jnp.zeros((128, 768), F32)
    for n in range(3):
        cols = pl.ds(n * 512, 512)
        gate = dot(trans_in, r.wgate[:, cols])
        up = dot(trans_in, r.wup[:, cols])
        d_hidden = r.dh[:, cols]
        sig = 1.0 / (1.0 + jnp.exp(-gate))
        d_gate = (d_hidden * up * sig * (1.0 + gate * (1.0 - sig))).astype(BF)
        d_up = (d_hidden * gate * sig).astype(BF)
        d_trans = d_trans + dot(d_gate, r.wgate[:, cols], 1, 1) + dot(d_up, r.wup[:, cols], 1, 1)
    d_res = r.cot[...].astype(F32) + layer_backward(d_trans, r.tg[...], trans_hat, trans_inverse)
    r.dres[...] = d_res
    d_res_t = d_res.T.astype(BF)
    r.drs[...] = d_res_t
    r.dr[me.tok] = d_res_t
    r.dk[...] = jnp.zeros_like(r.dk)
    r.dv[...] = jnp.zeros_like(r.dv)
    r.go[...] = jnp.zeros_like(r.go)
    r.wg[...] = jnp.zeros_like(r.wg)
    ds = gather_chain(w, me, r.drs, r.dr, 768)
    wo_own = r.wo[pl.ds(pl.multiple_of(h * 96, 96), 96)]

    def back(t):
        rows = pl.ds(pl.multiple_of(t * 128, 128), 128)
        d_att = dot(wo_own, r.dr[t]).astype(BF)
        d_att = jnp.concatenate([d_att, jnp.zeros((32, 128), BF)], axis=0)
        p = r.pt[t]
        dp = dot(r.v[...], d_att)
        pf = p.astype(F32)
        dsb = (pf * (dp - jnp.sum(pf * dp, axis=0, keepdims=True))).astype(BF)
        r.db[:, :, t] = dsb.reshape(16, 2, 32, 128)
        dqt = (dot(r.kt[...], dsb)[:96] * scale).astype(BF)
        r.dq[t, 0] = dqt
        r.zz[0:96, rows] = dqt
        r.dv[...] += dot(p, d_att.astype(F32).T.astype(BF))
        r.dk[...] += dot(dsb, r.q[rows])

    turns(ds)

    @pl.loop(0, 8)
    def _(t):
        back(t)

    mine = pl.ds(4 * me.core, 4)
    theirs = pl.ds(4 * (1 - me.core), 4)

    def bias_sum():
        c = w.go(r.db.at[:, :, theirs], r.db1, me.other_core())
        yield 1
        c.wait_recv()

        @pl.loop(0, 16)
        def _(n):
            r.s1[n] = (r.db[n, :, mine].astype(F32) + r.db1[n].astype(F32)).astype(BF)

        def done(total):
            r.bu[...] = total.astype(BF)

        yield from scatter_chain(w, me, r.s1, [getattr(r, "bd" + str(n)) for n in range(5)], done)
        c = w.go(r.bu.at[1 - me.core], r.bl.at[mine], me.other_core())
        r.bl[mine] = r.bu[me.core]
        yield 1
        c.wait_recv()
        fan = [w.go(r.bl.at[t], r.odb.at[me.tok], d) for t, d in toks]
        r.odb[me.tok] = r.bl[me.tok]
        yield 1
        for c in fan:
            c.wait_recv()

    bsum = bias_sum()
    step(bsum)
    dkt = (r.dk[...] * scale).T[:96].astype(BF)
    dvt = r.dv[...].T[:96].astype(BF)
    for t in range(8):
        r.dq[t, 1] = dkt[:, t * 128 : (t + 1) * 128]
        r.dq[t, 2] = dvt[:, t * 128 : (t + 1) * 128]
    r.zz[96:192] = dkt
    r.zz[192:288] = dvt
    step(bsum)
    moves = [w.go(r.dq.at[t], r.odq.at[:, me.tok], d) for t, d in toks]
    r.odq[:, me.tok] = r.dq[me.tok]

    @pl.loop(0, 8)
    def _(t):
        r.go[...] += dot(r.dr[t], r.att[t].astype(F32).T.astype(BF))

    for n in range(32):
        r.wg[n % 2, n // 2, 3, :, 0:96] = r.go[n * 24 : (n + 1) * 24].astype(BF)
    step(bsum)
    xf = r.xf[...].reshape(1024, 768)
    for s in range(3):
        g = dot(r.zz[s * 96 : (s + 1) * 96], xf)
        for te in range(8):
            part = g[:, te * 96 : (te + 1) * 96].astype(BF)
            for j in range(4):
                r.wg[j % 2, 2 * te + j // 2, s, :, 0:96] = part[j * 24 : (j + 1) * 24]
    step(bsum)
    tk = w.take(1)

    def turned():
        return w.copy(r.gt.at[pl.ds(0, 3)], r.owg.at[pl.ds(0, 3)], partner, tk)

    def weight_sum():
        c = w.go(r.wg.at[1 - me.core], r.wg1, me.other_core())
        yield 1
        c.wait_recv()
        r.ws[...] = (r.wg[me.core].astype(F32) + r.wg1[...].astype(F32)).astype(BF)

        def done(total):
            r.gt[...] = total.astype(BF)

        yield from scatter_chain(w, me, r.ws, [getattr(r, "bw" + str(n)) for n in range(5)], done)
        r.owg[3] = r.gt[3]

        @pl.when(other)
        def _():
            turned().start()

        @pl.when(jnp.logical_not(other))
        def _():
            r.owg[pl.ds(0, 3)] = r.gt[pl.ds(0, 3)]

    wsum = weight_sum()
    step(wsum)
    step(bsum)
    for c in moves:
        c.wait_recv()
    odq = r.odq[...].reshape(3, 768, 128)
    d_in_t = dot(r.wq[...], odq[0]) + dot(r.wk[...], odq[1]) + dot(r.wv[...], odq[2])
    for n in range(32):
        r.gs[n % 2, n // 2] = d_in_t[n * 24 : (n + 1) * 24].astype(BF)

    def single_sum():
        c = w.go(r.gs.at[1 - me.core], r.gs1, me.other_core())
        yield 1
        c.wait_recv()
        r.ss[...] = (r.gs[me.core].astype(F32) + r.gs1[...].astype(F32)).astype(BF)

        def done(total):
            r.ogs[...] = total

        yield from scatter_chain(w, me, r.ss, [getattr(r, "bg" + str(n)) for n in range(5)], done)

    gsum = single_sum()
    step(wsum)
    step(gsum)
    step(bsum)
    scaled, noisy_hat, noisy_inverse = layer_forward(r.noisy[...].astype(F32), r.ng[...])
    r.gn[...] = (
        r.dres[...] + layer_backward(d_in_t.T, r.ng[...], noisy_hat, noisy_inverse)
    ).astype(BF)
    turns(bsum, wsum, gsum)

    for n in range(8):
        r.gj[pl.ds(n, 32, stride=8)] = r.odb[n].astype(F32)
    r.p3[...] = jnp.zeros_like(r.p3)

    @pl.loop(0, 32)
    def _(j):
        g = r.gj[pl.ds(pl.multiple_of(j * 8, 8), 8)].astype(BF)
        r.p3[...] += dot(g, r.pr[j])

    def in_order(own, got, at):
        terms = []
        for k in range(4):
            d = lax.rem(at + 4 - k, 4)
            term = jnp.where(d == 0, own[...], jnp.zeros_like(own[...]))
            for j in (1, 2, 3):
                term = jnp.where(d == j, got[j - 1], term)
            terms.append(term)
        return (terms[0] + terms[1]) + (terms[2] + terms[3])

    def pair_weight_sum():
        c = w.go(r.p3, r.r0, me.other_core())
        yield 1
        c.wait_recv()
        r.p0[...] = r.p3[...] + r.r0[...]
        zs = [w.go(r.p0, r.r1.at[k - 1], me.around_z(k)) for k in (1, 2, 3)]
        yield 1
        for c in zs:
            c.wait_recv()
        r.p1[...] = in_order(r.p0, r.r1, me.z)
        ys = [w.go(r.p1, r.r2.at[k - 1], me.around_y(k)) for k in (1, 2, 3)]
        yield 1
        for c in ys:
            c.wait_recv()
        r.p2[...] = in_order(r.p1, r.r2, me.y)
        ts = [w.go(r.p2, r.r3.at[me.tok], d) for _, d in toks]
        r.r3[me.tok] = r.p2[...]
        yield 1
        for c in ts:
            c.wait_recv()
        total = r.r3[0]
        for k in range(1, 8):
            total = total + r.r3[k]
        r.opw[...] = total

    psum = pair_weight_sum()
    for n in range(4):
        step(psum)

        @pl.loop(n * 8, n * 8 + 8)
        def _(j):
            g = r.gj[pl.ds(pl.multiple_of(j * 8, 8), 8)].astype(BF)
            up = dot(g, r.wp[...], 0, 0)
            hat, inverse = layer_forward(r.pair[j].astype(F32), r.pg[...])[1:]
            r.gp[j] = layer_backward(up, r.pg[...], hat, inverse).astype(BF)

    turns(psum)

    @pl.when(other)
    def _():
        turned().wait()

    w.close()


def whole_block(*args):
    spaces = [VM] * 12 + [pl.BlockSpec(memory_space=pltpu.SMEM)]
    spaces += [pl.BlockSpec(memory_space=pl.ANY)] * 7
    return pl.pallas_call(
        block_kernel,
        out_shape=[jax.ShapeDtypeStruct(s, d) for s, d in OUT_SHAPES],
        in_specs=spaces,
        out_specs=[VM] * len(OUT_SHAPES),
        scratch_shapes=list(SCRATCH.values()),
        compiler_params=pltpu.CompilerParams(
            collective_id=0, has_side_effects=True, vmem_limit_bytes=62 << 20
        ),
    )(*args)


def per_device(
    noisy,
    single,
    pair,
    restype,
    chain,
    keymask,
    restype_table,
    norm_gain,
    pair_gain,
    trans_gain,
    w_query,
    w_key,
    w_value,
    w_out,
    w_pair,
    chain_weight,
    w_hidden_gate,
    w_hidden_up,
    w_down,
    cotangent,
):
    gn, ogs, gp, owg, opw = whole_block(
        noisy[0],
        single,
        jnp.transpose(pair, (1, 0, 2)),
        restype.reshape(1, 128),
        chain.reshape(8, 128),
        keymask.reshape(8, 128),
        restype_table,
        norm_gain.reshape(1, 768),
        pair_gain.reshape(1, 128),
        trans_gain.reshape(1, 768),
        w_pair.T,
        cotangent[0],
        chain_weight,
        w_query,
        w_key,
        w_value,
        w_out,
        w_hidden_gate,
        w_hidden_up,
        w_down,
    )
    grads = jnp.transpose(owg[:, :, :96].astype(F32), (0, 2, 1))
    return (
        gn[None],
        ogs.T,
        jnp.transpose(gp, (1, 0, 2)),
        grads[0],
        grads[1],
        grads[2],
        grads[3],
        opw.T,
    )


def solution(mesh):
    torus = Mesh(
        mesh.devices.reshape(4, 4, 2, 2, 4), ("copy_0", "copy_1", "copy_2", "tok_0", "tok_1")
    )
    return jax.shard_map(
        per_device,
        mesh=torus,
        in_specs=(
            P(COPY, TOK, None),
            P(TOK, None),
            P(TOK, COPY, None),
            P(TOK),
            P(),
            P(),
            P(),
            P(),
            P(),
            P(),
            P(),
            P(),
            P(),
            P(),
            P(),
            P(),
            P(),
            P(),
            P(),
            P(COPY, TOK, None),
        ),
        out_specs=(
            P(COPY, TOK, None),
            P(TOK, COPY),
            P(TOK, COPY, None),
            P(TOK, COPY),
            P(TOK, COPY),
            P(TOK, COPY),
            P(TOK, COPY),
            P(),
        ),
        check_vma=False,
    )
```

time: 460 us -> 170 us (0.37)
  waiting for transfers between devices: 212 us -> 0 us
  Pallas kernels: 0 us -> 159 us
  blocking collectives: 62.2 us -> 0 us
  matrix products: 57.8 us -> 0 us
  local copies, waits for them, and re-layouts: 48.1 us -> 9.21 us
  starting transfers between devices: 31.6 us -> 0 us
  other arithmetic: 29.9 us -> 0.01 us
  between operations: 14.7 us -> 0.7 us
    pallas_call x0 -> x1, Pallas kernels: none -> 159 us  [whole_block(): pl.pallas_call(block_kernel, out_shape=[jax.ShapeDtypeStruct(s, d) for s,...]
    all_to_all x5 -> x0, waiting for transfers between devices: 89.2 us -> none  [the longest x2 64.5 us: summed_rows(): lax.all_to_all(own.astype(jnp.bfloat16), far, 0, 0, tiled=True)]
    unnamed x3 -> x0, waiting for transfers between devices: 80.9 us -> none
    dot_general x27 -> x0, matrix products: 57.8 us -> none  [the longest x13 23.8 us: matmul(): return jnp.dot(left, right, preferred_element_type=jnp.float32)]
    all_gather x1 -> x0, waiting for transfers between devices: 42.2 us -> none  [sent_together(): filled, at, done = (lax.all_gather(both, axis, axis=dim, tiled=True), 0, [])]
    psum x5 -> x0, blocking collectives: 41.9 us -> none  [by_axis(): return functools.reduce(lax.psum, axes, shard)]
    all_to_all x5 -> x0, starting transfers between devices: 31.5 us -> none  [the longest x2 11.4 us: summed_on_arrival(): lax.all_to_all(blocks, axis, split_axis=0, concat_axis=0, tiled=True)]
    all_to_all x3 -> x0, blocking collectives: 20.3 us -> none  [the longest x2 14.9 us: summed_on_arrival(): lax.all_to_all(blocks, axis, split_axis=0, concat_axis=0, tiled=True)]
  transfers between devices with their start and end apart: 7 -> 0, of which waited for: 5 -> 0; matrix products, arithmetic and copies ran while one was open for 15% -> 0% of each run, Pallas kernels for 0% -> 0%
where the time goes in v2:
time: 170 us; the launch traced here: 169 us
  Pallas kernels  159 us (94%)
  local copies, waits for them, and re-layouts  9.21 us (5%)
    pallas_call x1, Pallas kernels, whole_block(): pl.pallas_call(block_kernel, out_shape=[jax.ShapeDtypeStruct(s, d) for s,...  159 us
    unnamed x17, local copies, waits for them, and re-layouts  7.43 us

profile of v2, /device:TPU:24, one launch (start us, length us, event | category | flops | bytes accessed | tf_op | source)
XLA Modules:
  0.0 168.5 jit_solution(18288981368643655249)
XLA Ops:
  0.6 0.0 copy-start.3
  0.6 0.0 copy-start.4
  0.7 2.6 %copy.31 = bf16[128,32,128]{2,0,1:T(8,128)(2,1)} copy(bf16[128,32,128]{2,1,0:T(8,128)(2,1)} %param.22) | data formatting | bytes 2097152 | tf_op args[2]
  3.3 0.0 copy-done.3
  3.3 0.6 reshape.37.refs_7_
  3.9 0.0 copy-done.4
  3.9 0.6 reshape.39.refs_9_
  4.4 158.6 %shard_map.251 = (bf16[128,768]{1,0:T(8,128)(2,1)}, f32[24,128]{1,0:T(8,128)}, bf16[32,128,128]{2,1,0:T(8,128)(2,1)}, bf16[4,24,128]{2,1,0:T(8,128)(2,1)}, f32[8,128]{1,0:T(8,128)}) custom-call(bf16[128,768]{1,0:T(8,128)(2,1)} %bitcast.27, bf16[128,768]{1,0:T(8,128)(2,1)} %refs_1_.1, bf16[32,128,128]{2,1,0:T(8,128)(2,1)} %bitcast.24, s32[1,128]{1,0:T(1,128)} %bitcast.34, ...), custom_call_target="tpu_custom_call" | custom-call | tf_op jit(solution)/shard_map/pallas_call | solution.py:685
  163.1 0.0 copy-start.1
  163.1 0.0 copy-start
  163.1 0.0 copy-start.2
  163.1 0.0 copy-start.5
  163.1 2.9 %copy.29 = bf16[128,32,128]{2,1,0:T(8,128)(2,1)} copy(bf16[128,32,128]{2,0,1:T(8,128)(2,1)} %bitcast.25) | data formatting | bytes 2097152
  166.0 0.0 copy-done.1
  166.0 0.6 slice_bitcast_fusion
  166.7 0.0 copy-done
  166.7 0.7 copy.35
  167.3 0.0 copy-done.2
  167.3 0.6 copy.36
  167.9 0.0 copy-done.5
  168.0 0.6 copy.37
  (1 shorter events, 0.0 us)
Async XLA Ops:
  0.6 2.6 %copy-start.3 = (f32[768]{0:T(1024)S(1)}, f32[768]{0:T(1024)}, u32[]{:S(2)}) copy-start(f32[768]{0:T(1024)} %param.27) | copy-start | bytes 9220
  0.6 3.2 %copy-start.4 = (f32[768]{0:T(1024)S(1)}, f32[768]{0:T(1024)}, u32[]{:S(2)}) copy-start(f32[768]{0:T(1024)} %param.29) | copy-start | bytes 9220
  163.1 3.0 %copy-start.1 = (bf16[4,24,128]{2,1,0:T(8,128)(2,1)S(1)}, bf16[4,24,128]{2,1,0:T(8,128)(2,1)}, u32[]{:S(2)}) copy-start(bf16[4,24,128]{2,1,0:T(8,128)(2,1)} %get-tuple-element.16) | copy-start | bytes 73732
  163.1 3.6 %copy-start = (bf16[128,768]{1,0:T(8,128)(2,1)S(1)}, bf16[128,768]{1,0:T(8,128)(2,1)}, u32[]{:S(2)}) copy-start(bf16[128,768]{1,0:T(8,128)(2,1)} %get-tuple-element.13) | copy-start | bytes 589828
  163.1 4.3 %copy-start.2 = (f32[24,128]{1,0:T(8,128)S(1)}, f32[24,128]{1,0:T(8,128)}, u32[]{:S(2)}) copy-start(f32[24,128]{1,0:T(8,128)} %get-tuple-element.14) | copy-start | bytes 36868
  163.1 4.8 %copy-start.5 = (f32[8,128]{1,0:T(8,128)S(1)}, f32[8,128]{1,0:T(8,128)}, u32[]{:S(2)}) copy-start(f32[8,128]{1,0:T(8,128)} %get-tuple-element.17) | copy-start | bytes 12292

commit v3 on v2

--- a/solution.py
+++ b/solution.py
@@ -140,39 +140,48 @@
     first = w.go(f.at[me.copy, theirs], f.at[me.copy, theirs], me.other_core())
     yield 1
     first.wait_recv()
-    chip = f.at[pl.ds(me.chip * 2, 2), mine]
+
+    def part(y, k):
+        return f.at[pl.ds((y * 4 + lax.rem(me.z + 4 - k, 4)) * 2, 2), mine]
+
+    def both_ways(k):
+        p = part(me.y, k)
+        return w.go(p, p, me.around_y(3)), w.go(p, p, me.around_y(1))
+
+    def to_core(p):
+        last.append(w.go(p, p, me.other_core()))
+
+    chip = part(me.y, 0)
     zs = [w.go(chip, chip, me.around_z(k)) for k in (1, 2, 3)]
+    rings = [both_ways(0)]
     last = [w.go(f.at[me.copy, mine], f.at[me.copy, mine], me.other_core())]
-    yield 1
-    for c in zs:
-        c.wait_recv()
-    row = f.at[pl.ds(me.y * 8, 8), mine]
-    left = w.go(row, row, me.around_y(3))
-    right = w.go(row, row, me.around_y(1))
-    for k in (1, 2, 3):
-        r = f.at[pl.ds((me.y * 4 + lax.rem(me.z + 4 - k, 4)) * 2, 2), mine]
-        last.append(w.go(r, r, me.other_core()))
-    lo = lax.rem(me.y + 3, 4) * 8
-    hi = lax.rem(me.y + 1, 4) * 8
-    op = lax.rem(me.y + 2, 4) * 8
-    yield 1
-    right.wait_recv()
-    r = f.at[pl.ds(lo, 4), mine]
-    a = w.go(r, r, me.around_y(1))
-    r = f.at[pl.ds(lo, 8), mine]
-    last.append(w.go(r, r, me.other_core()))
-    left.wait_recv()
-    r = f.at[pl.ds(hi + 4, 4), mine]
-    b = w.go(r, r, me.around_y(3))
-    r = f.at[pl.ds(hi, 8), mine]
-    last.append(w.go(r, r, me.other_core()))
-    yield 1
-    a.wait_recv()
-    r = f.at[pl.ds(op, 4), mine]
-    last.append(w.go(r, r, me.other_core()))
-    b.wait_recv()
-    r = f.at[pl.ds(op + 4, 4), mine]
-    last.append(w.go(r, r, me.other_core()))
+    lo = lax.rem(me.y + 3, 4)
+    hi = lax.rem(me.y + 1, 4)
+    op = lax.rem(me.y + 2, 4)
+    far = []
+    for k in range(4):
+        yield 1
+        if k < 3:
+            zs[k].wait_recv()
+            rings.append(both_ways(k + 1))
+            to_core(part(me.y, k + 1))
+        yield 1
+        left, right = rings[k]
+        right.wait_recv()
+        left.wait_recv()
+        if k % 2 == 0:
+            p = part(lo, k)
+            far.append(w.go(p, p, me.around_y(1)))
+        else:
+            p = part(hi, k)
+            far.append(w.go(p, p, me.around_y(3)))
+        to_core(part(lo, k))
+        to_core(part(hi, k))
+    yield 1
+    for k in range(4):
+        far[k].wait_recv()
+        to_core(part(op, k))
+    yield 1
     for c in last:
         c.wait_recv()
 
@@ -240,16 +249,14 @@
     return inverse * (scaled - first_moment - normed * second_moment)
 
 
-INPUTS = (
-    ("noisy", "single", "pair", "restype", "chain", "keymask", "table")
-    + ("ng", "pg", "tg", "wp", "cot", "cw")
-    + ("wq_h", "wk_h", "wv_h", "wo_h", "wg_h", "wu_h", "wd_h")
-)
+LOADED = ("noisy", "single", "restype", "table", "ng", "pair", "pg", "wp", "chain", "keymask")
+LOADED += ("wq", "wk", "wv", "cot", "wdown", "wo", "tg", "wgate", "wup")
+INPUTS = tuple(n + "_h" for n in LOADED) + ("cw",)
 OUTPUTS = ("gn", "ogs", "gp", "owg", "opw")
 OUT_SHAPES = (
     ((128, 768), BF),
     ((24, 128), F32),
-    ((32, 128, 128), BF),
+    ((128, 32, 128), BF),
     ((4, 24, 128), BF),
     ((8, 128), F32),
 )
@@ -262,9 +269,25 @@
     wgate=V((768, 1536), BF),
     wup=V((768, 1536), BF),
     wdown=V((1536, 768), BF),
-    load=pltpu.SemaphoreType.DMA((7,)),
-    send=pltpu.SemaphoreType.DMA((140,)),
-    recv=pltpu.SemaphoreType.DMA((140,)),
+    noisy=V((128, 768), BF),
+    single=V((128, 768), BF),
+    restype=V((1, 128), jnp.int32),
+    table=V((32, 768), BF),
+    ng=V((768,), F32),
+    pair=V((128, 32, 128), BF),
+    pg=V((1, 128), F32),
+    wp=V((8, 128), BF),
+    chain=V((8, 128), jnp.int32),
+    keymask=V((8, 128), jnp.int32),
+    cot=V((128, 768), BF),
+    tg=V((768,), F32),
+    pairs=V((32 * 136, 128), F32),
+    das=V((8, 96, 128), BF),
+    dat=V((8, 96, 128), BF),
+    g2=V((8, 4096), F32),
+    load=pltpu.SemaphoreType.DMA((19,)),
+    send=pltpu.SemaphoreType.DMA((180,)),
+    recv=pltpu.SemaphoreType.DMA((180,)),
     xs=V((128, 768), BF),
     xf=V((8, 128, 768), BF),
     pr=V((32, 128, 128), BF),
@@ -354,41 +377,53 @@
     def _():
         pl.semaphore_signal(barrier, inc=1, device_id=partner, device_id_type=MESH)
 
-    pairs = (
-        (r.wq_h, r.wq),
-        (r.wk_h, r.wk),
-        (r.wv_h, r.wv),
-        (r.wd_h, r.wdown),
-        (r.wo_h, r.wo),
-        (r.wg_h, r.wgate),
-        (r.wu_h, r.wup),
-    )
-    loads = [pltpu.make_async_copy(a, b, r.load.at[n]) for n, (a, b) in enumerate(pairs)]
-    for c in loads:
+    loads = {}
+    for n, name in enumerate(LOADED):
+        c = pltpu.make_async_copy(getattr(r, name + "_h"), getattr(r, name), r.load.at[n])
         c.start()
-
+        loads[name] = c
+
+    def ready(*names):
+        for name in names:
+            loads[name].wait()
+
+    ready("noisy", "single", "restype", "table", "ng")
+    gain = r.ng[...].reshape(1, 768)
     noisy_f = r.noisy[...].astype(F32)
     classes = lax.broadcasted_iota(jnp.int32, (32, 128), 0) == r.restype[...]
     classes = jnp.where(classes, 1.0, 0.0).astype(BF)
     condition = r.single[...].astype(F32) + dot(classes, r.table[...], 0, 0)
-    x = (layer_forward(noisy_f, r.ng[...])[0] + condition).astype(BF)
+    x = (layer_forward(noisy_f, gain)[0] + condition).astype(BF)
     r.xs[...] = x
     r.xf[me.tok] = x
+
+    ready("pair", "pg", "wp")
+
+    @pl.loop(0, 16)
+    def _(n):
+        for m in range(8):
+            i = n * 8 + m
+            r.pairs[pl.ds(i, 32, stride=136)] = r.pair[i].astype(F32)
+
+    def column(j):
+        return pl.ds(pl.multiple_of(j * 136, 8), 128)
+
+    @pl.loop(0, 8)
+    def _(n):
+        for m in range(4):
+            j = n * 4 + m
+            p = layer_forward(r.pairs[column(j)], r.pg[...])[0].astype(BF)
+            r.pr[j] = p
+            r.bj[pl.ds(pl.multiple_of(j * 8, 8), 8)] = dot(r.wp[...], p, 1, 1)
+
+    for n in range(8):
+        r.bt[n] = r.bj[pl.ds(n, 32, stride=8)].astype(BF)
     pl.semaphore_wait(barrier, len(peers) + jnp.where(other, 1, 0))
+    bs = bias_chain(w, me, r.bt, r.f, toks)
+    step(bs)
     xs = gather_chain(w, me, r.xs, r.xf, 128)
     step(xs)
-
-    @pl.loop(0, 32)
-    def _(j):
-        p = layer_forward(r.pair[j].astype(F32), r.pg[...])[0].astype(BF)
-        r.pr[j] = p
-        r.bj[pl.ds(pl.multiple_of(j * 8, 8), 8)] = dot(r.wp[...], p, 1, 1)
-
-    for n in range(8):
-        r.bt[n] = r.bj[pl.ds(n, 32, stride=8)].astype(BF)
-    bs = bias_chain(w, me, r.bt, r.f, toks)
-    step(bs)
-    step(xs)
+    ready("chain", "keymask")
     for t in range(8):
         code = jnp.where(r.keymask[t : t + 1] > 0, r.chain[t : t + 1], r.chain[t : t + 1] + 8)
         code = jnp.broadcast_to(code.astype(F32), (128, 128)).T
@@ -400,8 +435,7 @@
         r.ab[rows] = same
         r.bb[rows] = jnp.where(code >= 8, -1e30, 0.0)
     step(bs)
-    for c in loads[:3]:
-        c.wait()
+    ready("wq", "wk", "wv")
     row = lax.broadcasted_iota(jnp.int32, (768, 128), 0)
     col = lax.broadcasted_iota(jnp.int32, (768, 128), 1)
     pick = jnp.where((row == col + h * 96) & (col < 96), 1.0, 0.0).astype(BF)
@@ -414,17 +448,22 @@
 
     step(bs)
     step(xs)
-    loads[3].wait()
+    ready("cot", "wdown")
     r.dh[...] = dot(r.cot[...], r.wdown[...], 1, 1)
-    step(xs)
     step(bs)
-    for t in range(4):
-        project(me.zh * 4 + t)
     step(xs)
     step(bs)
     step(xs)
     for t in range(4):
+        project(me.zh * 4 + t)
+    step(bs)
+    step(xs)
+    step(bs)
+    step(xs)
+    step(bs)
+    for t in range(4):
         project((1 - me.zh) * 4 + t)
+    step(bs)
     r.vt[...] = r.v[...].T
     r.kt[...] = r.k[...].T
     turns(bs, xs)
@@ -457,10 +496,10 @@
     for s in range(7):
         att_copy(s, toks[s][0]).wait()
 
-    for c in loads[4:]:
-        c.wait()
+    ready("wo", "tg", "wgate", "wup")
+    trans_gain = r.tg[...].reshape(1, 768)
     residual = noisy_f + dot(r.attl[...].reshape(768, 128), r.wo[...], 0, 0)
-    scaled, trans_hat, trans_inverse = layer_forward(residual, r.tg[...])
+    scaled, trans_hat, trans_inverse = layer_forward(residual, trans_gain)
     trans_in = scaled.astype(BF)
     d_trans = jnp.zeros((128, 768), F32)
     for n in range(3):
@@ -472,22 +511,27 @@
         d_gate = (d_hidden * up * sig * (1.0 + gate * (1.0 - sig))).astype(BF)
         d_up = (d_hidden * gate * sig).astype(BF)
         d_trans = d_trans + dot(d_gate, r.wgate[:, cols], 1, 1) + dot(d_up, r.wup[:, cols], 1, 1)
-    d_res = r.cot[...].astype(F32) + layer_backward(d_trans, r.tg[...], trans_hat, trans_inverse)
+    d_res = r.cot[...].astype(F32) + layer_backward(d_trans, trans_gain, trans_hat, trans_inverse)
     r.dres[...] = d_res
+    d_att = dot(r.wo[...], d_res.astype(BF), 1, 1)
+    r.das[...] = d_att.astype(BF).reshape(8, 96, 128)
     d_res_t = d_res.T.astype(BF)
     r.drs[...] = d_res_t
     r.dr[me.tok] = d_res_t
+    fan = [w.go(r.das.at[t], r.dat.at[me.tok], d) for t, d in toks]
+    r.dat[me.tok] = r.das[me.tok]
+    ds = gather_chain(w, me, r.drs, r.dr, 768)
+    step(ds)
     r.dk[...] = jnp.zeros_like(r.dk)
     r.dv[...] = jnp.zeros_like(r.dv)
     r.go[...] = jnp.zeros_like(r.go)
     r.wg[...] = jnp.zeros_like(r.wg)
-    ds = gather_chain(w, me, r.drs, r.dr, 768)
-    wo_own = r.wo[pl.ds(pl.multiple_of(h * 96, 96), 96)]
+    for c in fan:
+        c.wait_recv()
 
     def back(t):
         rows = pl.ds(pl.multiple_of(t * 128, 128), 128)
-        d_att = dot(wo_own, r.dr[t]).astype(BF)
-        d_att = jnp.concatenate([d_att, jnp.zeros((32, 128), BF)], axis=0)
+        d_att = jnp.concatenate([r.dat[t], jnp.zeros((32, 128), BF)], axis=0)
         p = r.pt[t]
         dp = dot(r.v[...], d_att)
         pf = p.astype(F32)
@@ -499,11 +543,10 @@
         r.dv[...] += dot(p, d_att.astype(F32).T.astype(BF))
         r.dk[...] += dot(dsb, r.q[rows])
 
-    turns(ds)
-
-    @pl.loop(0, 8)
-    def _(t):
-        back(t)
+
+    @pl.loop(0, 4)
+    def _(n):
+        back(4 * (1 - me.core) + n)
 
     mine = pl.ds(4 * me.core, 4)
     theirs = pl.ds(4 * (1 - me.core), 4)
@@ -533,6 +576,14 @@
 
     bsum = bias_sum()
     step(bsum)
+    step(ds)
+
+    @pl.loop(0, 4)
+    def _(n):
+        back(4 * me.core + n)
+
+    step(bsum)
+    step(ds)
     dkt = (r.dk[...] * scale).T[:96].astype(BF)
     dvt = r.dv[...].T[:96].astype(BF)
     for t in range(8):
@@ -540,17 +591,9 @@
         r.dq[t, 2] = dvt[:, t * 128 : (t + 1) * 128]
     r.zz[96:192] = dkt
     r.zz[192:288] = dvt
-    step(bsum)
     moves = [w.go(r.dq.at[t], r.odq.at[:, me.tok], d) for t, d in toks]
     r.odq[:, me.tok] = r.dq[me.tok]
 
-    @pl.loop(0, 8)
-    def _(t):
-        r.go[...] += dot(r.dr[t], r.att[t].astype(F32).T.astype(BF))
-
-    for n in range(32):
-        r.wg[n % 2, n // 2, 3, :, 0:96] = r.go[n * 24 : (n + 1) * 24].astype(BF)
-    step(bsum)
     xf = r.xf[...].reshape(1024, 768)
     for s in range(3):
         g = dot(r.zz[s * 96 : (s + 1) * 96], xf)
@@ -559,6 +602,14 @@
             for j in range(4):
                 r.wg[j % 2, 2 * te + j // 2, s, :, 0:96] = part[j * 24 : (j + 1) * 24]
     step(bsum)
+    turns(ds)
+
+    @pl.loop(0, 8)
+    def _(t):
+        r.go[...] += dot(r.dr[t], r.att[t].astype(F32).T.astype(BF))
+
+    for n in range(32):
+        r.wg[n % 2, n // 2, 3, :, 0:96] = r.go[n * 24 : (n + 1) * 24].astype(BF)
     tk = w.take(1)
 
     def turned():
@@ -586,7 +637,6 @@
 
     wsum = weight_sum()
     step(wsum)
-    step(bsum)
     for c in moves:
         c.wait_recv()
     odq = r.odq[...].reshape(3, 768, 128)
@@ -606,23 +656,27 @@
         yield from scatter_chain(w, me, r.ss, [getattr(r, "bg" + str(n)) for n in range(5)], done)
 
     gsum = single_sum()
+    step(gsum)
+    step(bsum)
+    step(wsum)
+    step(gsum)
+    scaled, noisy_hat, noisy_inverse = layer_forward(r.noisy[...].astype(F32), gain)
+    r.gn[...] = (
+        r.dres[...] + layer_backward(d_in_t.T, gain, noisy_hat, noisy_inverse)
+    ).astype(BF)
     step(wsum)
     step(gsum)
     step(bsum)
-    scaled, noisy_hat, noisy_inverse = layer_forward(r.noisy[...].astype(F32), r.ng[...])
-    r.gn[...] = (
-        r.dres[...] + layer_backward(d_in_t.T, r.ng[...], noisy_hat, noisy_inverse)
-    ).astype(BF)
-    turns(bsum, wsum, gsum)
+    step(bsum)
+    step(wsum)
+    step(gsum)
+    turns(bsum)
 
     for n in range(8):
         r.gj[pl.ds(n, 32, stride=8)] = r.odb[n].astype(F32)
-    r.p3[...] = jnp.zeros_like(r.p3)
-
-    @pl.loop(0, 32)
-    def _(j):
-        g = r.gj[pl.ds(pl.multiple_of(j * 8, 8), 8)].astype(BF)
-        r.p3[...] += dot(g, r.pr[j])
+    for n in range(32):
+        r.g2[:, n * 128 : (n + 1) * 128] = r.gj[n * 8 : (n + 1) * 8]
+    r.p3[...] = dot(r.g2[...].astype(BF), r.pr[...].reshape(4096, 128))
 
     def in_order(own, got, at):
         terms = []
@@ -663,14 +717,22 @@
     for n in range(4):
         step(psum)
 
-        @pl.loop(n * 8, n * 8 + 8)
-        def _(j):
-            g = r.gj[pl.ds(pl.multiple_of(j * 8, 8), 8)].astype(BF)
-            up = dot(g, r.wp[...], 0, 0)
-            hat, inverse = layer_forward(r.pair[j].astype(F32), r.pg[...])[1:]
-            r.gp[j] = layer_backward(up, r.pg[...], hat, inverse).astype(BF)
-
-    turns(psum)
+        @pl.loop(n * 2, n * 2 + 2)
+        def _(b):
+            for m in range(4):
+                j = b * 4 + m
+                g = r.gj[pl.ds(pl.multiple_of(j * 8, 8), 8)].astype(BF)
+                up = dot(g, r.wp[...], 0, 0)
+                hat, inverse = layer_forward(r.pairs[column(j)], r.pg[...])[1:]
+                r.pairs[column(j)] = layer_backward(up, r.pg[...], hat, inverse)
+
+    @pl.loop(0, 16)
+    def _(n):
+        for m in range(8):
+            i = n * 8 + m
+            r.gp[i] = r.pairs[pl.ds(i, 32, stride=136)].astype(BF)
+
+    turns(psum, wsum, gsum)
 
     @pl.when(other)
     def _():
@@ -680,8 +742,8 @@
 
 
 def whole_block(*args):
-    spaces = [VM] * 12 + [pl.BlockSpec(memory_space=pltpu.SMEM)]
-    spaces += [pl.BlockSpec(memory_space=pl.ANY)] * 7
+    spaces = [pl.BlockSpec(memory_space=pl.ANY)] * len(LOADED)
+    spaces += [pl.BlockSpec(memory_space=pltpu.SMEM)]
     return pl.pallas_call(
         block_kernel,
         out_shape=[jax.ShapeDtypeStruct(s, d) for s, d in OUT_SHAPES],
@@ -719,30 +781,30 @@
     gn, ogs, gp, owg, opw = whole_block(
         noisy[0],
         single,
-        jnp.transpose(pair, (1, 0, 2)),
         restype.reshape(1, 128),
+        restype_table,
+        norm_gain,
+        pair,
+        pair_gain.reshape(1, 128),
+        w_pair.T,
         chain.reshape(8, 128),
         keymask.reshape(8, 128),
-        restype_table,
-        norm_gain.reshape(1, 768),
-        pair_gain.reshape(1, 128),
-        trans_gain.reshape(1, 768),
-        w_pair.T,
-        cotangent[0],
-        chain_weight,
         w_query,
         w_key,
         w_value,
+        cotangent[0],
+        w_down,
         w_out,
+        trans_gain,
         w_hidden_gate,
         w_hidden_up,
-        w_down,
+        chain_weight,
     )
     grads = jnp.transpose(owg[:, :, :96].astype(F32), (0, 2, 1))
     return (
         gn[None],
         ogs.T,
-        jnp.transpose(gp, (1, 0, 2)),
+        gp,
         grads[0],
         grads[1],
         grads[2],

time: 170 us -> 142 us (0.84)
  Pallas kernels: 159 us -> 134 us
  local copies, waits for them, and re-layouts: 9.21 us -> 6.4 us
    pallas_call x1, Pallas kernels: 159 us -> 134 us  [whole_block(): pl.pallas_call(block_kernel, out_shape=[jax.ShapeDtypeStruct(s, d) for s,...]
    unnamed x17 -> x6, local copies, waits for them, and re-layouts: 7.43 us -> 5.78 us
where the time goes in v3:
time: 142 us
  Pallas kernels  134 us (94%)
  local copies, waits for them, and re-layouts  6.4 us (5%)
    pallas_call x1, Pallas kernels, whole_block(): pl.pallas_call(block_kernel, out_shape=[jax.ShapeDtypeStruct(s, d) for s,...  134 us
    unnamed x6, local copies, waits for them, and re-layouts  5.78 us

profile of v3, /device:TPU:24, one launch (start us, length us, event | category | flops | bytes accessed | tf_op | source)
XLA Modules:
  0.0 141.8 jit_solution(2155328717812361078)
XLA Ops:
  0.6 134.0 %shard_map.251 = (bf16[128,768]{1,0:T(8,128)(2,1)}, f32[24,128]{1,0:T(8,128)}, bf16[128,32,128]{2,1,0:T(8,128)(2,1)}, bf16[4,24,128]{2,1,0:T(8,128)(2,1)}, f32[8,128]{1,0:T(8,128)}) custom-call(bf16[128,768]{1,0:T(8,128)(2,1)} %bitcast.21, bf16[128,768]{1,0:T(8,128)(2,1)} %refs_1_.1, s32[1,128]{1,0:T(1,128)} %bitcast.28, bf16[32,768]{1,0:T(8,128)(2,1)} %refs_3_.1, ...), custom_call_target="tpu_custom_call" | custom-call | tf_op jit(solution)/shard_map/pallas_call | solution.py:747
  134.6 0.7 convert_bitcast_fusion
  135.4 0.6 slice_bitcast_fusion
  136.0 0.0 copy-start
  136.0 1.6 %copy.32 = bf16[1,128,768]{2,1,0:T(8,128)(2,1)} copy(bf16[1,128,768]{2,1,0:T(8,128)(2,1)} %bitcast.20) | data formatting | bytes 393216
  137.6 1.3 copy.33
  138.9 2.3 %copy.34 = bf16[128,32,128]{2,1,0:T(8,128)(2,1)} copy(bf16[128,32,128]{2,1,0:T(8,128)(2,1)} %get-tuple-element.32) | data formatting | bytes 2097152
  141.2 0.0 copy-done
  141.2 0.6 copy.35
Async XLA Ops:
  136.0 5.2 %copy-start = (f32[8,128]{1,0:T(8,128)S(1)}, f32[8,128]{1,0:T(8,128)}, u32[]{:S(2)}) copy-start(f32[8,128]{1,0:T(8,128)} %get-tuple-element.17) | copy-start | bytes 12292

commit v4 on v3

--- a/solution.py
+++ b/solution.py
@@ -255,9 +255,9 @@
 OUTPUTS = ("gn", "ogs", "gp", "owg", "opw")
 OUT_SHAPES = (
     ((128, 768), BF),
-    ((24, 128), F32),
+    ((2, 24, 128), F32),
     ((128, 32, 128), BF),
-    ((4, 24, 128), BF),
+    ((3, 24, 128), BF),
     ((8, 128), F32),
 )
 V = pltpu.VMEM
@@ -316,19 +316,19 @@
     dv=V((1024, 128), F32),
     go=V((768, 96), F32),
     zz=V((288, 1024), BF),
-    wg=V((2, 16, 4, 24, 128), BF),
-    wg1=V((16, 4, 24, 128), BF),
-    ws=V((16, 4, 24, 128), BF),
-    gt=V((4, 24, 128), BF),
+    wg=V((2, 16, 3, 24, 128), BF),
+    wg1=V((16, 3, 24, 128), BF),
+    ws=V((16, 3, 24, 128), BF),
+    gt=V((3, 24, 128), BF),
     db1=V((16, 2, 4, 32, 128), BF),
     s1=V((16, 2, 4, 32, 128), BF),
     bu=V((2, 4, 32, 128), BF),
     bl=V((8, 32, 128), BF),
     odb=V((8, 32, 128), BF),
     gj=V((256, 128), F32),
-    gs=V((2, 16, 24, 128), BF),
-    gs1=V((16, 24, 128), BF),
-    ss=V((16, 24, 128), BF),
+    gs=V((2, 16, 2, 24, 128), BF),
+    gs1=V((16, 2, 24, 128), BF),
+    ss=V((16, 2, 24, 128), BF),
     p0=V((8, 128), F32),
     p1=V((8, 128), F32),
     p2=V((8, 128), F32),
@@ -338,7 +338,7 @@
     r2=V((3, 8, 128), F32),
     r3=V((8, 8, 128), F32),
 )
-for name, rest in (("bw", (4, 24, 128)), ("bd", (2, 4, 32, 128)), ("bg", (24, 128))):
+for name, rest in (("bw", (3, 24, 128)), ("bd", (2, 4, 32, 128)), ("bg", (2, 24, 128))):
     for at, ref in enumerate(scatter_scratch(rest)):
         SCRATCH[name + str(at)] = ref
 
@@ -526,6 +526,7 @@
     r.dv[...] = jnp.zeros_like(r.dv)
     r.go[...] = jnp.zeros_like(r.go)
     r.wg[...] = jnp.zeros_like(r.wg)
+    r.gs[...] = jnp.zeros_like(r.gs)
     for c in fan:
         c.wait_recv()
 
@@ -601,6 +602,35 @@
             part = g[:, te * 96 : (te + 1) * 96].astype(BF)
             for j in range(4):
                 r.wg[j % 2, 2 * te + j // 2, s, :, 0:96] = part[j * 24 : (j + 1) * 24]
+    tk = w.take(1)
+
+    def turned():
+        return w.copy(r.gt, r.owg, partner, tk)
+
+    def weight_sum():
+        c = w.go(r.wg.at[1 - me.core], r.wg1, me.other_core())
+        yield 1
+        c.wait_recv()
+        r.ws[...] = (r.wg[me.core].astype(F32) + r.wg1[...].astype(F32)).astype(BF)
+
+        def done(total):
+            r.gt[...] = total.astype(BF)
+
+        yield from scatter_chain(w, me, r.ws, [getattr(r, "bw" + str(n)) for n in range(5)], done)
+        @pl.when(other)
+        def _():
+            turned().start()
+
+        @pl.when(jnp.logical_not(other))
+        def _():
+            r.owg[...] = r.gt[...]
+
+    wsum = weight_sum()
+    step(wsum)
+    step(bsum)
+    step(ds)
+    step(wsum)
+    step(ds)
     step(bsum)
     turns(ds)
 
@@ -609,40 +639,15 @@
         r.go[...] += dot(r.dr[t], r.att[t].astype(F32).T.astype(BF))
 
     for n in range(32):
-        r.wg[n % 2, n // 2, 3, :, 0:96] = r.go[n * 24 : (n + 1) * 24].astype(BF)
-    tk = w.take(1)
-
-    def turned():
-        return w.copy(r.gt.at[pl.ds(0, 3)], r.owg.at[pl.ds(0, 3)], partner, tk)
-
-    def weight_sum():
-        c = w.go(r.wg.at[1 - me.core], r.wg1, me.other_core())
-        yield 1
-        c.wait_recv()
-        r.ws[...] = (r.wg[me.core].astype(F32) + r.wg1[...].astype(F32)).astype(BF)
-
-        def done(total):
-            r.gt[...] = total.astype(BF)
-
-        yield from scatter_chain(w, me, r.ws, [getattr(r, "bw" + str(n)) for n in range(5)], done)
-        r.owg[3] = r.gt[3]
-
-        @pl.when(other)
-        def _():
-            turned().start()
-
-        @pl.when(jnp.logical_not(other))
-        def _():
-            r.owg[pl.ds(0, 3)] = r.gt[pl.ds(0, 3)]
-
-    wsum = weight_sum()
+        r.gs[n % 2, n // 2, 1, :, 0:96] = r.go[n * 24 : (n + 1) * 24].astype(BF)
     step(wsum)
+    step(bsum)
     for c in moves:
         c.wait_recv()
     odq = r.odq[...].reshape(3, 768, 128)
     d_in_t = dot(r.wq[...], odq[0]) + dot(r.wk[...], odq[1]) + dot(r.wv[...], odq[2])
     for n in range(32):
-        r.gs[n % 2, n // 2] = d_in_t[n * 24 : (n + 1) * 24].astype(BF)
+        r.gs[n % 2, n // 2, 0] = d_in_t[n * 24 : (n + 1) * 24].astype(BF)
 
     def single_sum():
         c = w.go(r.gs.at[1 - me.core], r.gs1, me.other_core())
@@ -666,10 +671,6 @@
     ).astype(BF)
     step(wsum)
     step(gsum)
-    step(bsum)
-    step(bsum)
-    step(wsum)
-    step(gsum)
     turns(bsum)
 
     for n in range(8):
@@ -716,6 +717,8 @@
     psum = pair_weight_sum()
     for n in range(4):
         step(psum)
+        if n in (1, 2):
+            step(gsum)
 
         @pl.loop(n * 2, n * 2 + 2)
         def _(b):
@@ -753,6 +756,65 @@
         compiler_params=pltpu.CompilerParams(
             collective_id=0, has_side_effects=True, vmem_limit_bytes=62 << 20
         ),
+    )(*args)
+
+
+def results_kernel(gn, ogs, gp, owg, opw, *rest):
+    outs, (vgn, vgp, vogs, vowg, vopw, sem) = rest[:8], rest[8:]
+    ogn, osingle, ogp, oq, ok, ov, oo, opair = outs
+    ins = [pltpu.make_async_copy(gp.at[pl.ds(n * 32, 32)], vgp.at[n], sem.at[n]) for n in range(4)]
+    ins.append(pltpu.make_async_copy(gn, vgn, sem.at[4]))
+    small = [
+        pltpu.make_async_copy(a, b, sem.at[5 + n])
+        for n, (a, b) in enumerate(((ogs, vogs), (owg, vowg), (opw, vopw)))
+    ]
+    for c in ins + small:
+        c.start()
+    back = [
+        pltpu.make_async_copy(vgp.at[n], ogp.at[pl.ds(n * 32, 32)], sem.at[8 + n])
+        for n in range(4)
+    ]
+    back.append(pltpu.make_async_copy(vgn, ogn, sem.at[12]))
+    for a, b in zip(ins, back):
+        a.wait()
+        b.start()
+    for c in small:
+        c.wait()
+    osingle[...] = vogs[0]
+    for n, o in enumerate((oq, ok, ov)):
+        o[...] = vowg[n, :, 0:96].astype(F32)
+    oo[...] = vogs[1, :, 0:96]
+    opair[...] = vopw[...]
+    for c in back:
+        c.wait()
+
+
+def results(*args):
+    grad = jax.ShapeDtypeStruct((24, 96), F32)
+    anywhere = pl.BlockSpec(memory_space=pl.ANY)
+    return pl.pallas_call(
+        results_kernel,
+        out_shape=[
+            jax.ShapeDtypeStruct((128, 768), BF),
+            jax.ShapeDtypeStruct((24, 128), F32),
+            jax.ShapeDtypeStruct((128, 32, 128), BF),
+            grad,
+            grad,
+            grad,
+            grad,
+            jax.ShapeDtypeStruct((8, 128), F32),
+        ],
+        in_specs=[anywhere] * 5,
+        out_specs=[anywhere, VM, anywhere, VM, VM, VM, VM, VM],
+        scratch_shapes=[
+            V((128, 768), BF),
+            V((4, 32, 32, 128), BF),
+            V((2, 24, 128), F32),
+            V((3, 24, 128), BF),
+            V((8, 128), F32),
+            pltpu.SemaphoreType.DMA((13,)),
+        ],
+        compiler_params=pltpu.CompilerParams(vmem_limit_bytes=60 << 20),
     )(*args)
 
 
@@ -778,7 +840,7 @@
     w_down,
     cotangent,
 ):
-    gn, ogs, gp, owg, opw = whole_block(
+    parts = whole_block(
         noisy[0],
         single,
         restype.reshape(1, 128),
@@ -800,17 +862,8 @@
         w_hidden_up,
         chain_weight,
     )
-    grads = jnp.transpose(owg[:, :, :96].astype(F32), (0, 2, 1))
-    return (
-        gn[None],
-        ogs.T,
-        gp,
-        grads[0],
-        grads[1],
-        grads[2],
-        grads[3],
-        opw.T,
-    )
+    gn, gsingle, gp, gq, gk, gv, gout, gpw = results(*parts)
+    return gn[None], gsingle.T, gp, gq.T, gk.T, gv.T, gout.T, gpw.T
 
 
 def solution(mesh):

time: 142 us -> 128 us (0.901)
  Pallas kernels: 134 us -> 126 us
  local copies, waits for them, and re-layouts: 6.4 us -> 0 us
    pallas_call x1, Pallas kernels: 134 us -> 124 us  [whole_block(): pl.pallas_call(block_kernel, out_shape=[jax.ShapeDtypeStruct(s, d) for s,...]
    unnamed x6 -> x0, local copies, waits for them, and re-layouts: 5.78 us -> none
    pallas_call x0 -> x1, Pallas kernels: none -> 2.71 us  [results(): pl.pallas_call(results_kernel, out_shape=[jax.ShapeDtypeStruct((128, 768)...]
where the time goes in v4:
time: 128 us; the launch traced here: 127 us
  Pallas kernels  126 us (98%)
    pallas_call x1, Pallas kernels, whole_block(): pl.pallas_call(block_kernel, out_shape=[jax.ShapeDtypeStruct(s, d) for s,...  124 us
    pallas_call x1, Pallas kernels, results(): pl.pallas_call(results_kernel, out_shape=[jax.ShapeDtypeStruct((128, 768)...  2.71 us

profile of v4, /device:TPU:24, one launch (start us, length us, event | category | flops | bytes accessed | tf_op | source)
XLA Modules:
  0.0 127.1 jit_solution(7754292402158097937)
XLA Ops:
  0.6 123.6 %shard_map.251 = (bf16[128,768]{1,0:T(8,128)(2,1)}, f32[2,24,128]{2,1,0:T(8,128)}, bf16[128,32,128]{2,1,0:T(8,128)(2,1)}, bf16[3,24,128]{2,1,0:T(8,128)(2,1)}, f32[8,128]{1,0:T(8,128)}) custom-call(bf16[128,768]{1,0:T(8,128)(2,1)} %bitcast.14, bf16[128,768]{1,0:T(8,128)(2,1)} %refs_1_.1, s32[1,128]{1,0:T(1,128)} %bitcast.19, bf16[32,768]{1,0:T(8,128)(2,1)} %refs_3_.1, ...), custom_call_target="tpu_custom_call" | custom-call | tf_op jit(solution)/shard_map/pallas_call | solution.py:750
  124.3 2.7 %shard_map.252 = (bf16[128,768]{1,0:T(8,128)(2,1)}, f32[24,128]{1,0:T(8,128)}, bf16[128,32,128]{2,1,0:T(8,128)(2,1)}, f32[24,96]{1,0:T(8,128)}, f32[24,96]{1,0:T...) custom-call(bf16[128,768]{1,0:T(8,128)(2,1)} %get-tuple-element.21.gn, ...), custom_call_target="tpu_custom_call" | custom-call | tf_op jit(solution)/shard_map/pallas_call | solution.py:795

commit v5 on v4

--- a/solution.py
+++ b/solution.py
@@ -78,6 +78,7 @@
     def close(self):
         for c in self.open:
             c.wait_send()
+        self.open = []
 
 
 def turns(*chains):
@@ -252,7 +253,7 @@
 LOADED = ("noisy", "single", "restype", "table", "ng", "pair", "pg", "wp", "chain", "keymask")
 LOADED += ("wq", "wk", "wv", "cot", "wdown", "wo", "tg", "wgate", "wup")
 INPUTS = tuple(n + "_h" for n in LOADED) + ("cw",)
-OUTPUTS = ("gn", "ogs", "gp", "owg", "opw")
+OUTPUTS = ("gn_o", "ogs", "gp_o", "owg", "opw")
 OUT_SHAPES = (
     ((128, 768), BF),
     ((2, 24, 128), F32),
@@ -285,7 +286,10 @@
     das=V((8, 96, 128), BF),
     dat=V((8, 96, 128), BF),
     g2=V((8, 4096), F32),
+    gn=V((128, 768), BF),
+    gp=V((128, 32, 128), BF),
     load=pltpu.SemaphoreType.DMA((19,)),
+    store=pltpu.SemaphoreType.DMA((2,)),
     send=pltpu.SemaphoreType.DMA((180,)),
     recv=pltpu.SemaphoreType.DMA((180,)),
     xs=V((128, 768), BF),
@@ -452,18 +456,16 @@
     r.dh[...] = dot(r.cot[...], r.wdown[...], 1, 1)
     step(bs)
     step(xs)
-    step(bs)
+    step(bs, 2)
     step(xs)
     for t in range(4):
         project(me.zh * 4 + t)
-    step(bs)
+    step(bs, 2)
     step(xs)
-    step(bs)
+    step(bs, 3)
     step(xs)
-    step(bs)
     for t in range(4):
         project((1 - me.zh) * 4 + t)
-    step(bs)
     r.vt[...] = r.v[...].T
     r.kt[...] = r.k[...].T
     turns(bs, xs)
@@ -735,12 +737,21 @@
             i = n * 8 + m
             r.gp[i] = r.pairs[pl.ds(i, 32, stride=136)].astype(BF)
 
+    w.close()
+    stores = [
+        pltpu.make_async_copy(r.gn, r.gn_o, r.store.at[0]),
+        pltpu.make_async_copy(r.gp, r.gp_o, r.store.at[1]),
+    ]
+    for c in stores:
+        c.start()
     turns(psum, wsum, gsum)
 
     @pl.when(other)
     def _():
         turned().wait()
 
+    for c in stores:
+        c.wait()
     w.close()
 
 
@@ -751,7 +762,7 @@
         block_kernel,
         out_shape=[jax.ShapeDtypeStruct(s, d) for s, d in OUT_SHAPES],
         in_specs=spaces,
-        out_specs=[VM] * len(OUT_SHAPES),
+        out_specs=[spaces[0], VM, spaces[0], VM, VM],
         scratch_shapes=list(SCRATCH.values()),
         compiler_params=pltpu.CompilerParams(
             collective_id=0, has_side_effects=True, vmem_limit_bytes=62 << 20

time: 128 us -> 121 us (0.945)
  Pallas kernels: 126 us -> 119 us
    pallas_call x1, Pallas kernels: 124 us -> 116 us  [whole_block(): pl.pallas_call(block_kernel, out_shape=[jax.ShapeDtypeStruct(s, d) for s,...]
where the time goes in v5:
time: 121 us; the launch traced here: 120 us
  Pallas kernels  119 us (98%)
    pallas_call x1, Pallas kernels, whole_block(): pl.pallas_call(block_kernel, out_shape=[jax.ShapeDtypeStruct(s, d) for s,...  116 us
    pallas_call x1, Pallas kernels, results(): pl.pallas_call(results_kernel, out_shape=[jax.ShapeDtypeStruct((128, 768)...  2.71 us

profile of v5, /device:TPU:24, one launch (start us, length us, event | category | flops | bytes accessed | tf_op | source)
XLA Modules:
  0.0 119.8 jit_solution(10934142552874094326)
XLA Ops:
  0.6 116.3 %shard_map.251 = (bf16[128,768]{1,0:T(8,128)(2,1)}, f32[2,24,128]{2,1,0:T(8,128)}, bf16[128,32,128]{2,1,0:T(8,128)(2,1)}, bf16[3,24,128]{2,1,0:T(8,128)(2,1)}, f32[8,128]{1,0:T(8,128)}) custom-call(bf16[128,768]{1,0:T(8,128)(2,1)} %bitcast.14, bf16[128,768]{1,0:T(8,128)(2,1)} %refs_1_.1, s32[1,128]{1,0:T(1,128)} %bitcast.19, bf16[32,768]{1,0:T(8,128)(2,1)} %refs_3_.1, ...), custom_call_target="tpu_custom_call" | custom-call | tf_op jit(solution)/shard_map/pallas_call | solution.py:761
  117.0 2.7 %shard_map.252 = (bf16[128,768]{1,0:T(8,128)(2,1)}, f32[24,128]{1,0:T(8,128)}, bf16[128,32,128]{2,1,0:T(8,128)(2,1)}, f32[24,96]{1,0:T(8,128)}, f32[24,96]{1,0:T...) custom-call(bf16[128,768]{1,0:T(8,128)(2,1)} %get-tuple-element.21.gn, ...), custom_call_target="tpu_custom_call" | custom-call | tf_op jit(solution)/shard_map/pallas_call | solution.py:806
